TPU v7x, 512 devices: a whole 4x4x16 slice. The times are simulated.
512 devices in a mesh: lat: 128 (over y, z, x_hi), lon: 4 (over x_lo, core).
Axes of the slice: x: 4 (x_hi: 2, x_lo: 2; x = x_hi * 2 + x_lo), y: 4, z: 16, core: 2. Of those that a mesh axis runs over, the one named last changes fastest.
Arguments:
- grid_state: bfloat16 [256, 720, 640], P('lat', 'lon'), may hold values from -6 to 6
- conv_weight: float32 [3, 3, 640], replicated, may hold values from -2.4 to 2.4
- spectral_gain: float32 [2, 256, 640], P(None, None, 'lon'), may hold values from -4 to 4
- spectral_weight: bfloat16 [2, 640, 640], P(None, None, 'lon'), may hold values from -0.125 to 0.125
- norm_gain: float32 [640], replicated, may hold values from 0.1 to 1.9
- expand_weight: bfloat16 [640, 1280], replicated, may hold values from -0.25 to 0.25
- reduce_weight: bfloat16 [1280, 640], replicated, may hold values from -0.15625 to 0.15625
Outputs:
- block_output: bfloat16 [256, 720, 640], P('lat', 'lon')
All inputs are finite; a program needn't handle non-finite values.
Results may differ from a plain program's by a relative error of at most 0.015.
Values may be sent and summed in bfloat16 or wider, within the bound.
A program may use at most 64 MiB of HBM per device.

v0:
```python
import math

import jax
import jax.numpy as jnp
from jax import lax
from jax.sharding import PartitionSpec as P

M = 256


norm_eps = 1e-06
underflow_cut = -60.0
degree_block = 16


def padded_2(value, sides, width, wrap):
    for axis, dim in sides:
        count, length = (lax.axis_size(axis), value.shape[dim])
        up = [(i, (i + 1) % count) for i in range(count if wrap else count - 1)]
        down = [(j, i) for i, j in up]
        last = lax.slice_in_dim(value, length - width, length, axis=dim)
        initial = lax.slice_in_dim(value, 0, width, axis=dim)
        before = lax.ppermute(last, axis, up)
        after = lax.ppermute(initial, axis, down)
        value = jnp.concatenate([before, value, after], axis=dim)
    return value


def joined_along(parts, dim):
    parts = jnp.moveaxis(parts, 0, dim)
    dims = parts.shape
    return parts.reshape(*dims[:dim], dims[dim] * dims[dim + 1], *dims[dim + 2 :])


def from_everyone(value, axis):
    copies = jnp.broadcast_to(value, (lax.axis_size(axis), *value.shape))
    return lax.all_to_all(copies, axis, split_axis=0, concat_axis=0, tiled=True)


def gathered_copies(value, axis, dim):
    return joined_along(from_everyone(value, axis), dim)


def legendre_table(orders, lat_total, degree_count):
    colatitude = (jnp.arange(lat_total, dtype=jnp.float32) + 0.5) * (math.pi / lat_total)
    cosines = jnp.cos(colatitude)
    sine_values = jnp.sin(colatitude)
    rank_values = jnp.arange(1, degree_count + 1, dtype=jnp.int32)
    rank_float = rank_values.astype(jnp.float32)
    log_terms = 0.5 * jnp.log((2.0 * rank_float + 1.0) / (2.0 * rank_float))
    log_norm = jnp.sum(
        jnp.where(rank_values[None, :] <= orders[:, None], log_terms[None, :], jnp.float32(0.0)),
        axis=1,
    )
    order_float = orders.astype(jnp.float32)[:, None]
    log_start = (
        -0.5 * math.log(4.0 * math.pi)
        + log_norm[:, None]
        + order_float * jnp.log(sine_values)[None, :]
    )
    start_value = jnp.where(
        log_start > underflow_cut, jnp.exp(jnp.maximum(log_start, underflow_cut)), jnp.float32(0.0)
    )

    def advance_block(totals, block_start):
        previous, earlier = totals
        rows_out = []
        for inner in range(degree_block):
            degree = block_start + inner
            degree_float = degree.astype(jnp.float32)
            raise_coef = jnp.sqrt(
                jnp.maximum(4.0 * degree_float * degree_float - 1.0, 0.0)
                / jnp.maximum(degree_float * degree_float - order_float * order_float, 1.0)
            )
            lower_coef = jnp.sqrt(
                jnp.maximum((degree_float - 1.0) ** 2 - order_float * order_float, 0.0)
                / jnp.maximum(4.0 * (degree_float - 1.0) ** 2 - 1.0, 1.0)
            )
            recurred = raise_coef * (cosines[None, :] * previous - lower_coef * earlier)
            current = jnp.where(
                degree < orders[:, None],
                jnp.float32(0.0),
                jnp.where(degree == orders[:, None], start_value, recurred),
            )
            earlier = previous
            previous = current
            rows_out.append(current)
        return ((previous, earlier), jnp.stack(rows_out, axis=0))

    blank = jnp.zeros((orders.shape[0], lat_total), jnp.float32)
    starts = jnp.arange(0, degree_count, degree_block, dtype=jnp.int32)
    unused, table_blocks = lax.scan(advance_block, (blank, blank), starts)
    return table_blocks.reshape(degree_count, orders.shape[0], lat_total)


def quadrature(lat_total):
    colatitude = (jnp.arange(lat_total, dtype=jnp.float32) + 0.5) * (math.pi / lat_total)
    return 2.0 * math.pi * math.pi / lat_total * jnp.sin(colatitude)


def fourier_table(longitudes, lon_total, mode_count):
    mode_index = jnp.arange(mode_count, dtype=jnp.int32)
    phase_index = longitudes[:, None] * mode_index[None, :] % lon_total
    angles = phase_index.astype(jnp.float32) * (2.0 * math.pi / lon_total)
    return (jnp.stack([jnp.cos(angles), -jnp.sin(angles)], axis=1) / lon_total).astype(jnp.bfloat16)


def synthesis_table(longitudes, lon_total, mode_count):
    mode_index = jnp.arange(mode_count, dtype=jnp.int32)
    phase_index = mode_index[:, None] * longitudes[None, :] % lon_total
    angles = phase_index.astype(jnp.float32) * (2.0 * math.pi / lon_total)
    doubling = jnp.where(mode_index == 0, 1.0, 2.0).astype(jnp.float32)[:, None]
    return jnp.stack([doubling * jnp.cos(angles), -doubling * jnp.sin(angles)], axis=0).astype(
        jnp.bfloat16
    )


def shards(
    grid_state, conv_weight, spectral_gain, spectral_weight, norm_gain, expand_weight, reduce_weight
):
    lat_rows, sector_width, channel_total = grid_state.shape
    lat_count = lax.axis_size("lat")
    lon_count = lax.axis_size("lon")
    lat_total = lat_rows * lat_count
    lon_total = sector_width * lon_count
    mode_count = M
    order_share = mode_count // lat_count
    channel_share = channel_total // lon_count
    lat_position = lax.axis_index("lat")
    wrapped = padded_2(grid_state, (("lon", 1),), 1, True)
    padded = padded_2(wrapped, (("lat", 0),), 1, False)
    padded_wide = padded.astype(jnp.float32)
    filtered = jnp.zeros((lat_rows, sector_width, channel_total), jnp.float32)
    for row_shift in range(3):
        for col_shift in range(3):
            filtered = (
                filtered
                + conv_weight[row_shift, col_shift]
                * padded_wide[
                    row_shift : row_shift + lat_rows, col_shift : col_shift + sector_width
                ]
            )
    first_section = (grid_state.astype(jnp.float32) + jax.nn.gelu(filtered)).astype(jnp.bfloat16)
    gathered = lax.all_to_all(first_section, "lon", split_axis=2, concat_axis=1, tiled=True)
    forward_table = fourier_table(jnp.arange(lon_total, dtype=jnp.int32), lon_total, mode_count)
    spectrum = jnp.einsum(
        "tpc,prm->tmrc", gathered, forward_table, preferred_element_type=jnp.float32
    ).astype(jnp.bfloat16)
    cycle_spectrum = lax.all_to_all(spectrum, "lat", split_axis=1, concat_axis=0, tiled=True)
    orders = lat_position * order_share + jnp.arange(order_share, dtype=jnp.int32)
    legendre = legendre_table(orders, lat_total, mode_count)
    analysis_table = (legendre * quadrature(lat_total)[None, None, :]).astype(jnp.bfloat16)
    coefficients = jnp.einsum(
        "lmt,tmrc->lmrc", analysis_table, cycle_spectrum, preferred_element_type=jnp.float32
    )
    gain_real = spectral_gain[0][:, None, :]
    gain_imag = spectral_gain[1][:, None, :]
    coef_real = coefficients[:, :, 0, :]
    coef_imag = coefficients[:, :, 1, :]
    gained = jnp.stack(
        [
            gain_real * coef_real - gain_imag * coef_imag,
            gain_real * coef_imag + gain_imag * coef_real,
        ],
        axis=2,
    ).astype(jnp.bfloat16)
    blank = jnp.zeros((mode_count * order_share, channel_share), jnp.float32)
    portion = gathered_copies(gained, "lon", 3)
    width_part = portion.shape[3]
    weight_rows = lax.slice_in_dim(spectral_weight, 0, width_part, axis=1)
    real_part = portion[:, :, 0, :].reshape(-1, width_part)
    imag_part = portion[:, :, 1, :].reshape(-1, width_part)
    real_sum = (
        blank
        + jnp.dot(real_part, weight_rows[0], preferred_element_type=jnp.float32)
        - jnp.dot(imag_part, weight_rows[1], preferred_element_type=jnp.float32)
    )
    imag_sum = (
        blank
        + jnp.dot(real_part, weight_rows[1], preferred_element_type=jnp.float32)
        + jnp.dot(imag_part, weight_rows[0], preferred_element_type=jnp.float32)
    )
    mixed = jnp.stack(
        [
            real_sum.reshape(mode_count, order_share, channel_share),
            imag_sum.reshape(mode_count, order_share, channel_share),
        ],
        axis=2,
    ).astype(jnp.bfloat16)
    synthesis_legendre = legendre.astype(jnp.bfloat16)
    cycle_modes = jnp.einsum(
        "lmt,lmrc->tmrc", synthesis_legendre, mixed, preferred_element_type=jnp.float32
    ).astype(jnp.bfloat16)
    band_modes = lax.all_to_all(cycle_modes, "lat", split_axis=0, concat_axis=1, tiled=True)
    inverse_table = synthesis_table(jnp.arange(lon_total, dtype=jnp.int32), lon_total, mode_count)
    all_lons = jnp.einsum(
        "tmrc,rmp->tpc", band_modes, inverse_table, preferred_element_type=jnp.float32
    )
    spectral_out = lax.all_to_all(
        all_lons.astype(jnp.bfloat16), "lon", split_axis=1, concat_axis=2, tiled=True
    ).astype(all_lons.dtype)
    second_section = (first_section.astype(jnp.float32) + spectral_out).astype(jnp.bfloat16)
    second_wide = second_section.astype(jnp.float32)
    scale_values = lax.rsqrt(jnp.mean(second_wide * second_wide, axis=-1, keepdims=True) + norm_eps)
    normed = (second_wide * norm_gain * scale_values).astype(jnp.bfloat16)
    flat_rows = normed.reshape(-1, channel_total)
    hidden = jax.nn.gelu(
        jnp.dot(flat_rows, expand_weight, preferred_element_type=jnp.float32)
    ).astype(jnp.bfloat16)
    update = jnp.dot(hidden, reduce_weight, preferred_element_type=jnp.float32)
    block_output = (second_wide.reshape(-1, channel_total) + update).astype(jnp.bfloat16)
    return block_output.reshape(lat_rows, sector_width, channel_total)


def solution(mesh):
    return jax.shard_map(
        shards,
        mesh=mesh,
        in_specs=(
            P("lat", "lon", None),
            P(),
            P(None, None, "lon"),
            P(None, None, "lon"),
            P(),
            P(),
            P(),
        ),
        out_specs=P("lat", "lon", None),
        check_vma=False,
    )
```

profile of v0, /device:TPU:1, one launch (start us, length us, event | category | flops | bytes accessed | tf_op | source)
XLA Modules:
  0.0 384.5 jit_solution(18043150537942124979)
XLA Ops:
  1.2 4.5 %collective-permute-start = (bf16[2,1,640]{2,1,0:T(2,128)(2,1)S(1)}, bf16[2,1,640]{2,1,0:T(2,128)(2,1)S(1)}, u32[]{:S(2)}, u32[]{:S(2)}) collective-permute-start(bf16[2,1,640]{2,1,0:T(2,128)(2,1)S(1)} %get-tuple-element.533), channel_id=1, source_target_pairs={{0,1},{1,2},{2,3},{3,0},{4,5},{5,6},{6,7},{7,4},{8,9},{9,10},{10,1... | collective-permute-start | bytes 7688 | tf_op jit(solution)/shard_map/ppermute | solution.py:23
  5.7 6.2 %collective-permute-start.1 = (bf16[2,1,640]{2,1,0:T(2,128)(2,1)S(1)}, bf16[2,1,640]{2,1,0:T(2,128)(2,1)S(1)}, u32[]{:S(2)}, u32[]{:S(2)}) collective-permute-start(bf16[2,1,640]{2,1,0:T(2,128)(2,1)S(1)} %get-tuple-element.534), channel_id=1, source_target_pairs={{1,0},{2,1},{3,2},{0,3},{5,4},{6,5},{7,6},{4,7},{9,8},{10,9},{11,1... | collective-permute-start | bytes 7688 | tf_op jit(solution)/shard_map/ppermute | solution.py:24
  13.1 2.1 collective-permute-start.2
  15.2 1.3 collective-permute-start.3
  16.5 4.3 %sine_negate_fusion = (f32[720,1,256]{2,0,1:T(8,128)}, f32[720,1,256]{2,0,1:T(8,128)}) fusion(), kind=kLoop, calls=%fused_computation.182 | loop fusion | flops 1843200 | bytes 1474560 | tf_op jit(solution)/shard_map/neg | solution.py:105
  20.8 3.9 %collective-permute-done.3 = bf16[1,182,640]{2,1,0:T(8,128)(2,1)S(1)} collective-permute-done((bf16[1,182,640]{2,1,0:T(8,128)(2,1)S(1)}, bf16[1,182,640]{2,1,0:T(8,128)(2,1)S(1)}, u32[]{:S(2)}, u32[]{:S(2)}) %collective-permute-start.3) | collective-permute-done | bytes 232992 | tf_op jit(solution)/shard_map/ppermute | solution.py:24
  26.0 1.8 copy.70
  27.7 10.6 %all-to-all-start = ((bf16[2,180,640]{1,0,2:T(2,128)(2,1)}), bf16[2,180,640]{1,0,2:T(2,128)(2,1)S(1)}, u32[]{:S(2)}, u32[]{:S(2)}) async-start(bf16[2,180,640]{1,0,2:T(2,128)(2,1)} %copy.70), calls=%async_computation | async-start | bytes 1310720 | tf_op jit(solution)/shard_map/all_to_all | solution.py:144
  38.5 9.1 %all-to-all-done = bf16[2,180,640]{1,0,2:T(2,128)(2,1)S(1)} async-done(((bf16[2,180,640]{1,0,2:T(2,128)(2,1)}), bf16[2,180,640]{1,0,2:T(2,128)(2,1)S(1)}, u32[]{:S(2)}, u32[]{:S(2)}) %all-to-all-start) | async-done | bytes 460832 | tf_op jit(solution)/shard_map/all_to_all | solution.py:144
  48.6 1.8 fusion.56
  51.5 16.9 %all-to-all-start.1 = ((bf16[2,256,2,160]{3,0,2,1:T(2,128)(2,1)}), bf16[2,256,2,160]{3,0,2,1:T(2,128)(2,1)S(1)}, u32[]{:S(2)}, u32[]{:S(2)}) async-start(bf16[2,256,2,160]{3,0,2,1:T(2,128)(2,1)} %copy.73), calls=%async_computation.1 | async-start | bytes 1048576 | tf_op jit(solution)/shard_map/all_to_all | solution.py:149
  68.4 201.7 %while.21 = (s32[]{:T(128)}, f32[2,256]{1,0:T(2,128)S(1)}, f32[2,256]{1,0:T(2,128)S(1)}, f32[16,16,2,256]{3,2,1,0:T(2,128)S(1)}, s32[16]{0:T(128)S(1)}, /*index=...) while((s32[]{:T(128)}, f32[2,256]{1,0:T(2,128)S(1)}, ...), condition=%wide.region_2.3_spmd.clone.clone.clone.clone, body=%wide.region_1.2_spmd.clone.clone.clone.clone.sunk | while | flops 92737 | bytes 279792 | solution.py:92
  271.3 19.9 %all_to_all.68 = bf16[4,256,2,2,160]{1,4,3,2,0:T(8,128)(2,1)S(1)} all-to-all(bf16[4,256,2,2,160]{1,4,3,2,0:T(8,128)(2,1)S(1)} %broadcast_in_dim.453), channel_id=1, replica_groups=mesh['lat'=128,'lon'=4] {'lon'}, dimensions={0} | all-to-all | bytes 2621440 | tf_op jit(solution)/shard_map/all_to_all | solution.py:37
  291.4 1.8 copy.79
  293.2 2.1 reshape_squeeze.6
  298.9 1.4 fusion.57
  305.6 18.3 %all-to-all-start.3 = ((bf16[256,2,2,160]{3,2,1,0:T(2,128)(2,1)}), bf16[256,2,2,160]{3,2,1,0:T(2,128)(2,1)S(1)}, u32[]{:S(2)}, u32[]{:S(2)}) async-start(bf16[256,2,2,160]{3,2,1,0:T(2,128)(2,1)} %copy.86), calls=%async_computation.3 | async-start | bytes 1048576 | tf_op jit(solution)/shard_map/all_to_all | solution.py:194
  324.0 4.1 %multiply_convert_fusion.1 = (bf16[1,256,720]{1,2,0:T(8,128)(2,1)S(1)}, bf16[1,256,720]{1,2,0:T(8,128)(2,1)}) fusion(f32[256]{0:T(256)S(1)} %fusion.123, f32[256]{0:T(256)S(1)} %compare_select_fusion.2), kind=kLoop, calls=%fused_computation.187 | loop fusion | flops 2396160 | bytes 739328 | tf_op jit(solution)/shard_map/convert.10
  328.1 27.1 %all-to-all-done.3 = bf16[256,2,2,160]{3,2,1,0:T(2,128)(2,1)S(1)} async-done(((bf16[256,2,2,160]{3,2,1,0:T(2,128)(2,1)}), bf16[256,2,2,160]{3,2,1,0:T(2,128)(2,1)S(1)}, u32[]{:S(2)}, u32[]{:S(2)}) %all-to-all-start.3) | async-done | bytes 327712 | tf_op jit(solution)/shard_map/all_to_all | solution.py:194
  355.5 1.5 fusion.54
  358.0 16.8 %all_to_all.69 = bf16[2,720,160]{2,0,1:T(2,128)(2,1)S(1)} all-to-all(bf16[2,720,160]{2,0,1:T(2,128)(2,1)S(1)} %copy.89), channel_id=1, replica_groups=mesh['lat'=128,'lon'=4] {'lon'}, dimensions={1} | all-to-all | bytes 921600 | tf_op jit(solution)/shard_map/all_to_all | solution.py:199
  375.1 1.9 reshape.1013
  377.0 1.5 multiply_reduce_fusion
  379.8 3.4 fusion.53
  (891 shorter events, 68.3 us)
Async XLA Ops:
  0.0 379.8 %copy-start = (bf16[1280,640]{1,0:T(8,128)(2,1)S(1)}, bf16[1280,640]{1,0:T(8,128)(2,1)}, u32[]{:S(2)}) copy-start(bf16[1280,640]{1,0:T(8,128)(2,1)} %param.15) | copy-start | bytes 4915204
  1.2 11.7 %collective-permute-start = (bf16[2,1,640]{2,1,0:T(2,128)(2,1)S(1)}, bf16[2,1,640]{2,1,0:T(2,128)(2,1)S(1)}, u32[]{:S(2)}, u32[]{:S(2)}) collective-permute-start(bf16[2,1,640]{2,1,0:T(2,128)(2,1)S(1)} %get-tuple-element.533), channel_id=1, source_target_pairs={{0,1},{1,2},{2,3},{3,0},{4,5},{5,6},{6,7},{7,4},{8,9},{9,10},{10,1... | collective-permute-start | bytes 7688 | tf_op jit(solution)/shard_map/ppermute | solution.py:23
  5.7 7.2 %collective-permute-start.1 = (bf16[2,1,640]{2,1,0:T(2,128)(2,1)S(1)}, bf16[2,1,640]{2,1,0:T(2,128)(2,1)S(1)}, u32[]{:S(2)}, u32[]{:S(2)}) collective-permute-start(bf16[2,1,640]{2,1,0:T(2,128)(2,1)S(1)} %get-tuple-element.534), channel_id=1, source_target_pairs={{1,0},{2,1},{3,2},{0,3},{5,4},{6,5},{7,6},{4,7},{9,8},{10,9},{11,1... | collective-permute-start | bytes 7688 | tf_op jit(solution)/shard_map/ppermute | solution.py:24
  13.1 7.7 %collective-permute-start.2 = (bf16[1,182,640]{2,1,0:T(8,128)(2,1)S(1)}, bf16[1,182,640]{2,1,0:T(8,128)(2,1)S(1)}, u32[]{:S(2)}, u32[]{:S(2)}) collective-permute-start(bf16[1,182,640]{2,1,0:T(8,128)(2,1)S(1)} %get-tuple-element.531), channel_id=1, source_target_pairs={{0,4},{4,8},{8,12},{12,16},{16,20},{20,24},{24,28},{28,32},{32,36}... | collective-permute-start | bytes 698888 | tf_op jit(solution)/shard_map/ppermute | solution.py:23
  15.2 9.5 %collective-permute-start.3 = (bf16[1,182,640]{2,1,0:T(8,128)(2,1)S(1)}, bf16[1,182,640]{2,1,0:T(8,128)(2,1)S(1)}, u32[]{:S(2)}, u32[]{:S(2)}) collective-permute-start(bf16[1,182,640]{2,1,0:T(8,128)(2,1)S(1)} %get-tuple-element.532), channel_id=1, source_target_pairs={{4,0},{8,4},{12,8},{16,12},{20,16},{24,20},{28,24},{32,28},{36,32}... | collective-permute-start | bytes 698888 | tf_op jit(solution)/shard_map/ppermute | solution.py:24
  16.5 8.3 %copy-start.2 = (bf16[2,180,640]{2,0,1:T(2,128)(2,1)S(1)}, bf16[2,180,640]{2,0,1:T(2,128)(2,1)}, u32[]{:S(2)}) copy-start(bf16[2,180,640]{2,0,1:T(2,128)(2,1)} %param.9) | copy-start | bytes 1382404
  25.9 22.1 %copy-start.1 = (bf16[2,180,640]{2,1,0:T(8,128)(2,1)}, bf16[2,180,640]{2,1,0:T(8,128)(2,1)S(1)}, u32[]{:S(2)}) copy-start(bf16[2,180,640]{2,1,0:T(8,128)(2,1)S(1)} %fusion.67) | copy-start | bytes 1382404
  27.7 19.8 %all-to-all-start = ((bf16[2,180,640]{1,0,2:T(2,128)(2,1)}), bf16[2,180,640]{1,0,2:T(2,128)(2,1)S(1)}, u32[]{:S(2)}, u32[]{:S(2)}) async-start(bf16[2,180,640]{1,0,2:T(2,128)(2,1)} %copy.70), calls=%async_computation | async-start | bytes 1310720 | tf_op jit(solution)/shard_map/all_to_all | solution.py:144
  48.5 19.9 %copy-start.5 = (f32[16,16,2,256]{3,2,1,0:T(2,128)S(1)}, f32[16,16,2,256]{3,2,1,0:T(2,128)}, u32[]{:S(2)}) copy-start(f32[16,16,2,256]{3,2,1,0:T(2,128)} %custom-call.3) | copy-start | bytes 1572868
  51.5 218.7 %all-to-all-start.1 = ((bf16[2,256,2,160]{3,0,2,1:T(2,128)(2,1)}), bf16[2,256,2,160]{3,0,2,1:T(2,128)(2,1)S(1)}, u32[]{:S(2)}, u32[]{:S(2)}) async-start(bf16[2,256,2,160]{3,0,2,1:T(2,128)(2,1)} %copy.73), calls=%async_computation.1 | async-start | bytes 1048576 | tf_op jit(solution)/shard_map/all_to_all | solution.py:149
  68.4 201.8 %copy-start.7 = (f32[2,256,160]{1,2,0:T(8,128)S(1)}, f32[2,256,160]{1,2,0:T(8,128)}, u32[]{:S(2)}) copy-start(f32[2,256,160]{1,2,0:T(8,128)} %param.11) | copy-start | bytes 983044
  270.1 1.0 copy-start.6
  291.3 3.9 %copy-start.3 = (bf16[2,640,160]{1,2,0:T(8,128)(2,1)S(1)}, bf16[2,640,160]{1,2,0:T(8,128)(2,1)}, u32[]{:S(2)}) copy-start(bf16[2,640,160]{1,2,0:T(8,128)(2,1)} %param.12) | copy-start | bytes 1228804
  298.8 3.5 copy-start.4
  305.6 49.5 %all-to-all-start.3 = ((bf16[256,2,2,160]{3,2,1,0:T(2,128)(2,1)}), bf16[256,2,2,160]{3,2,1,0:T(2,128)(2,1)S(1)}, u32[]{:S(2)}, u32[]{:S(2)}) async-start(bf16[256,2,2,160]{3,2,1,0:T(2,128)(2,1)} %copy.86), calls=%async_computation.3 | async-start | bytes 1048576 | tf_op jit(solution)/shard_map/all_to_all | solution.py:194
  377.0 2.6 copy-start.8
where the time goes:
time: 387 us; the launch traced here: 384 us
  loops' own time  154 us (40%)
  starting transfers between devices  59.8 us (15%)
  other arithmetic  50.4 us (13%)
  waiting for transfers between devices  40.1 us (10%)
  blocking collectives  36.7 us (9%)
  local copies, waits for them, and re-layouts  31.1 us (8%)
  matrix products  12.2 us (3%)
    another operation x1, loops' own time, legendre_table(): unused, table_blocks = lax.scan(advance_block, (blank, blank), starts)  154 us
    all_to_all x1, waiting for transfers between devices, shards(): lax.all_to_all(cycle_modes, 'lat', split_axis=0, concat_axis=1, tiled=True)  27.1 us
    while x240, other arithmetic  21 us
    all_to_all x1, blocking collectives, from_everyone(): return lax.all_to_all(copies, axis, split_axis=0, concat_axis=0, tiled=True)  19.9 us
    all_to_all x1, starting transfers between devices, shards(): lax.all_to_all(cycle_modes, 'lat', split_axis=0, concat_axis=1, tiled=True)  18.3 us
    all_to_all x1, starting transfers between devices, shards(): lax.all_to_all(spectrum, 'lat', split_axis=1, concat_axis=0, tiled=True)  16.9 us
    all_to_all x1, blocking collectives, shards(): lax.all_to_all(all_lons.astype(jnp.bfloat16), 'lon', split_axis=1, concat...  16.8 us
    eq x256, other arithmetic, advance_block(): degree == orders[:, None]  11.4 us
  transfers between devices with their start and end apart: 7, of which 3 were waited for; matrix products, arithmetic and copies ran while one was open for 15% of the time, Pallas kernels for 0%

commit v1 on v0

v1 whole, which is shorter than its diff:
```python
import functools
import math

import jax
import jax.numpy as jnp
import numpy as np
from jax import lax
from jax.experimental import pallas as pl
from jax.experimental.pallas import tpu as pltpu
from jax.sharding import PartitionSpec as P

M = 256


norm_eps = 1e-06
underflow_cut = -60.0


def padded_2(value, sides, width, wrap):
    for axis, dim in sides:
        count, length = (lax.axis_size(axis), value.shape[dim])
        up = [(i, (i + 1) % count) for i in range(count if wrap else count - 1)]
        down = [(j, i) for i, j in up]
        last = lax.slice_in_dim(value, length - width, length, axis=dim)
        initial = lax.slice_in_dim(value, 0, width, axis=dim)
        before = lax.ppermute(last, axis, up)
        after = lax.ppermute(initial, axis, down)
        value = jnp.concatenate([before, value, after], axis=dim)
    return value


def joined_along(parts, dim):
    parts = jnp.moveaxis(parts, 0, dim)
    dims = parts.shape
    return parts.reshape(*dims[:dim], dims[dim] * dims[dim + 1], *dims[dim + 2 :])


def from_everyone(value, axis):
    copies = jnp.broadcast_to(value, (lax.axis_size(axis), *value.shape))
    return lax.all_to_all(copies, axis, split_axis=0, concat_axis=0, tiled=True)


def gathered_copies(value, axis, dim):
    return joined_along(from_everyone(value, axis), dim)


def latitude_rows(lat_total):
    theta = (np.arange(lat_total) + 0.5) * (math.pi / lat_total)
    rank = np.arange(1, lat_total + 1)
    rows = np.stack(
        [
            np.cos(theta),
            np.log(np.sin(theta)),
            2.0 * math.pi * math.pi / lat_total * np.sin(theta),
            0.5 * np.log((2.0 * rank + 1.0) / (2.0 * rank)),
        ]
    )
    return np.concatenate([rows, np.zeros_like(rows)]).astype(np.float32)


def legendre_fill(order, rows_ref, raise_ref, lower_ref, table_ref):
    degrees, width = table_ref.shape
    order_float = order.astype(jnp.float32)
    cosine = rows_ref[0:1, :]
    log_sine = rows_ref[1:2, :]
    rank = lax.broadcasted_iota(jnp.int32, (1, width), 1) + 1
    log_norm = jnp.sum(jnp.where(rank <= order, rows_ref[3:4, :], 0.0), axis=1, keepdims=True)
    log_start = -0.5 * math.log(4.0 * math.pi) + log_norm + order_float * log_sine
    start = jnp.where(log_start > underflow_cut, jnp.exp(jnp.maximum(log_start, underflow_cut)), 0.0)
    degree = lax.broadcasted_iota(jnp.int32, (degrees, width), 0).astype(jnp.float32)
    raise_coef = jnp.sqrt(
        jnp.maximum(4.0 * degree * degree - 1.0, 0.0)
        / jnp.maximum(degree * degree - order_float * order_float, 1.0)
    )
    below = degree - 1.0
    lower_coef = jnp.sqrt(
        jnp.maximum(below * below - order_float * order_float, 0.0)
        / jnp.maximum(4.0 * below * below - 1.0, 1.0)
    )
    raise_ref[...] = raise_coef * cosine
    lower_ref[...] = raise_coef * lower_coef

    def advance(degree_now, carried):
        previous, earlier = carried
        row = pl.ds(degree_now, 1)
        recurred = raise_ref[row, :] * previous - lower_ref[row, :] * earlier
        current = jnp.where(degree_now == order, start, recurred)
        table_ref[row, :] = current
        return current, previous

    blank = 0.0 * raise_ref[0:1, :]
    lax.fori_loop(0, degrees, advance, (blank, blank), unroll=8)


def legendre_kernel(order_count, rows_ref, analysis_ref, synthesis_ref, raise_ref, lower_ref, table_ref):
    order = lax.axis_index("lat") * order_count + pl.program_id(0)
    legendre_fill(order, rows_ref, raise_ref, lower_ref, table_ref)
    table = table_ref[...]
    synthesis_ref[...] = table.astype(jnp.bfloat16)
    analysis_ref[...] = (table * rows_ref[2:3, :]).astype(jnp.bfloat16)


def legendre_tables(order_count, lat_total, degree_count):
    square = (degree_count, lat_total)
    block = pl.BlockSpec((None, *square), lambda i: (i, 0, 0))
    return pl.pallas_call(
        functools.partial(legendre_kernel, order_count),
        grid=(order_count,),
        in_specs=[pl.BlockSpec((8, lat_total), lambda i: (0, 0))],
        out_specs=[block, block],
        out_shape=[jax.ShapeDtypeStruct((order_count, *square), jnp.bfloat16)] * 2,
        scratch_shapes=[pltpu.VMEM(square, jnp.float32)] * 3,
        name="legendre",
    )(jnp.asarray(latitude_rows(lat_total)))


def fourier_tables(lon_total, mode_count):
    phase = np.outer(np.arange(lon_total), np.arange(mode_count)) % lon_total
    angles = phase * (2.0 * math.pi / lon_total)
    forward = np.stack([np.cos(angles), -np.sin(angles)], axis=1) / lon_total
    doubling = np.where(np.arange(mode_count) == 0, 1.0, 2.0)
    inverse = np.stack([np.cos(angles).T, -np.sin(angles).T]) * doubling[None, :, None]
    return (
        jnp.asarray(forward.astype(np.float32).astype(jnp.bfloat16)),
        jnp.asarray(inverse.astype(np.float32).astype(jnp.bfloat16)),
    )


def shards(
    grid_state, conv_weight, spectral_gain, spectral_weight, norm_gain, expand_weight, reduce_weight
):
    lat_rows, sector_width, channel_total = grid_state.shape
    lat_count = lax.axis_size("lat")
    lon_count = lax.axis_size("lon")
    lat_total = lat_rows * lat_count
    lon_total = sector_width * lon_count
    mode_count = M
    order_share = mode_count // lat_count
    channel_share = channel_total // lon_count
    wrapped = padded_2(grid_state, (("lon", 1),), 1, True)
    padded = padded_2(wrapped, (("lat", 0),), 1, False)
    padded_wide = padded.astype(jnp.float32)
    filtered = jnp.zeros((lat_rows, sector_width, channel_total), jnp.float32)
    for row_shift in range(3):
        for col_shift in range(3):
            filtered = (
                filtered
                + conv_weight[row_shift, col_shift]
                * padded_wide[
                    row_shift : row_shift + lat_rows, col_shift : col_shift + sector_width
                ]
            )
    first_section = (grid_state.astype(jnp.float32) + jax.nn.gelu(filtered)).astype(jnp.bfloat16)
    gathered = lax.all_to_all(first_section, "lon", split_axis=2, concat_axis=1, tiled=True)
    forward_table, inverse_table = fourier_tables(lon_total, mode_count)
    spectrum = jnp.einsum(
        "tpc,prm->tmrc", gathered, forward_table, preferred_element_type=jnp.float32
    ).astype(jnp.bfloat16)
    cycle_spectrum = lax.all_to_all(spectrum, "lat", split_axis=1, concat_axis=0, tiled=True)
    analysis_table, synthesis_legendre = legendre_tables(order_share, lat_total, mode_count)
    coefficients = jnp.einsum(
        "mlt,tmrc->lmrc", analysis_table, cycle_spectrum, preferred_element_type=jnp.float32
    )
    gain_real = spectral_gain[0][:, None, :]
    gain_imag = spectral_gain[1][:, None, :]
    coef_real = coefficients[:, :, 0, :]
    coef_imag = coefficients[:, :, 1, :]
    gained = jnp.stack(
        [
            gain_real * coef_real - gain_imag * coef_imag,
            gain_real * coef_imag + gain_imag * coef_real,
        ],
        axis=2,
    ).astype(jnp.bfloat16)
    blank = jnp.zeros((mode_count * order_share, channel_share), jnp.float32)
    portion = gathered_copies(gained, "lon", 3)
    width_part = portion.shape[3]
    weight_rows = lax.slice_in_dim(spectral_weight, 0, width_part, axis=1)
    real_part = portion[:, :, 0, :].reshape(-1, width_part)
    imag_part = portion[:, :, 1, :].reshape(-1, width_part)
    real_sum = (
        blank
        + jnp.dot(real_part, weight_rows[0], preferred_element_type=jnp.float32)
        - jnp.dot(imag_part, weight_rows[1], preferred_element_type=jnp.float32)
    )
    imag_sum = (
        blank
        + jnp.dot(real_part, weight_rows[1], preferred_element_type=jnp.float32)
        + jnp.dot(imag_part, weight_rows[0], preferred_element_type=jnp.float32)
    )
    mixed = jnp.stack(
        [
            real_sum.reshape(mode_count, order_share, channel_share),
            imag_sum.reshape(mode_count, order_share, channel_share),
        ],
        axis=2,
    ).astype(jnp.bfloat16)
    cycle_modes = jnp.einsum(
        "mlt,lmrc->tmrc", synthesis_legendre, mixed, preferred_element_type=jnp.float32
    ).astype(jnp.bfloat16)
    band_modes = lax.all_to_all(cycle_modes, "lat", split_axis=0, concat_axis=1, tiled=True)
    all_lons = jnp.einsum(
        "tmrc,rmp->tpc", band_modes, inverse_table, preferred_element_type=jnp.float32
    )
    spectral_out = lax.all_to_all(
        all_lons.astype(jnp.bfloat16), "lon", split_axis=1, concat_axis=2, tiled=True
    ).astype(all_lons.dtype)
    second_section = (first_section.astype(jnp.float32) + spectral_out).astype(jnp.bfloat16)
    second_wide = second_section.astype(jnp.float32)
    scale_values = lax.rsqrt(jnp.mean(second_wide * second_wide, axis=-1, keepdims=True) + norm_eps)
    normed = (second_wide * norm_gain * scale_values).astype(jnp.bfloat16)
    flat_rows = normed.reshape(-1, channel_total)
    hidden = jax.nn.gelu(
        jnp.dot(flat_rows, expand_weight, preferred_element_type=jnp.float32)
    ).astype(jnp.bfloat16)
    update = jnp.dot(hidden, reduce_weight, preferred_element_type=jnp.float32)
    block_output = (second_wide.reshape(-1, channel_total) + update).astype(jnp.bfloat16)
    return block_output.reshape(lat_rows, sector_width, channel_total)


def solution(mesh):
    return jax.shard_map(
        shards,
        mesh=mesh,
        in_specs=(
            P("lat", "lon", None),
            P(),
            P(None, None, "lon"),
            P(None, None, "lon"),
            P(),
            P(),
            P(),
        ),
        out_specs=P("lat", "lon", None),
        check_vma=False,
    )
```

time: 387 us -> 205 us (0.53)
  loops' own time: 154 us -> 0 us
  blocking collectives: 36.7 us -> 96.7 us
  other arithmetic: 50.4 us -> 3.16 us
  starting transfers between devices: 59.8 us -> 31.4 us
  local copies, waits for them, and re-layouts: 31.1 us -> 19.9 us
  waiting for transfers between devices: 40.1 us -> 34.3 us
  Pallas kernels: 0 us -> 5.8 us
    another operation x1 -> x0, loops' own time: 154 us -> none  [legendre_table(): unused, table_blocks = lax.scan(advance_block, (blank, blank), starts)]
    all_to_all x0 -> x2, blocking collectives: none -> 57.1 us  [the longest x1 38.4 us: shards(): lax.all_to_all(cycle_modes, 'lat', split_axis=0, concat_axis=1, tiled=True)]
    all_to_all x2 -> x0, waiting for transfers between devices: 36.2 us -> none  [the longest x1 27.1 us: shards(): lax.all_to_all(cycle_modes, 'lat', split_axis=0, concat_axis=1, tiled=True)]
    all_to_all x2 -> x0, starting transfers between devices: 28.9 us -> none  [the longest x1 18.3 us: shards(): lax.all_to_all(cycle_modes, 'lat', split_axis=0, concat_axis=1, tiled=True)]
    all_to_all x1, waiting for transfers between devices: 0.01 us -> 25.4 us  [shards(): lax.all_to_all(spectrum, 'lat', split_axis=1, concat_axis=0, tiled=True)]
    while x240 -> x0, other arithmetic: 21 us -> none
    eq x256 -> x0, other arithmetic: 11.4 us -> none  [advance_block(): degree == orders[:, None]]
    dynamic_slice x16 -> x0, local copies, waits for them, and re-layouts: 9.25 us -> none  [legendre_table(): unused, table_blocks = lax.scan(advance_block, (blank, blank), starts)]
  transfers between devices with their start and end apart: 7 -> 5, of which waited for: 3 -> 4; matrix products, arithmetic and copies ran while one was open for 15% -> 0% of each run, Pallas kernels for 0% -> 3%
where the time goes in v1:
time: 205 us; the launch traced here: 204 us
  blocking collectives  96.7 us (47%)
  waiting for transfers between devices  34.3 us (17%)
  starting transfers between devices  31.4 us (15%)
  local copies, waits for them, and re-layouts  19.9 us (10%)
  matrix products  12.5 us (6%)
  Pallas kernels  5.8 us (3%)
  other arithmetic  3.16 us (2%)
    all_to_all x1, blocking collectives, shards(): lax.all_to_all(cycle_modes, 'lat', split_axis=0, concat_axis=1, tiled=True)  38.4 us
    all_to_all x1, waiting for transfers between devices, shards(): lax.all_to_all(spectrum, 'lat', split_axis=1, concat_axis=0, tiled=True)  25.4 us
    all_to_all x1, blocking collectives, from_everyone(): return lax.all_to_all(copies, axis, split_axis=0, concat_axis=0, tiled=True)  22.8 us
    all_to_all x1, blocking collectives, shards(): lax.all_to_all(first_section, 'lon', split_axis=2, concat_axis=1, tiled=T...  18.7 us
    all_to_all x1, starting transfers between devices, shards(): lax.all_to_all(spectrum, 'lat', split_axis=1, concat_axis=0, tiled=True)  17 us
    all_to_all x1, blocking collectives, shards(): lax.all_to_all(all_lons.astype(jnp.bfloat16), 'lon', split_axis=1, concat...  16.8 us
    ppermute x2, starting transfers between devices, padded_2(): after = lax.ppermute(initial, axis, down)  7.46 us
    ppermute x2, starting transfers between devices, padded_2(): before = lax.ppermute(last, axis, up)  6.96 us
  transfers between devices with their start and end apart: 5, of which 4 were waited for; matrix products, arithmetic and copies ran while one was open for 0% of the time, Pallas kernels for 3%

profile of v1, /device:TPU:1, one launch (start us, length us, event | category | flops | bytes accessed | tf_op | source)
XLA Modules:
  0.0 204.1 jit_solution(10378045567995268220)
XLA Ops:
  0.0 1.2 copy.38
  1.2 4.5 %collective-permute-start = (bf16[2,1,640]{2,1,0:T(2,128)(2,1)S(1)}, bf16[2,1,640]{2,1,0:T(2,128)(2,1)S(1)}, u32[]{:S(2)}, u32[]{:S(2)}) collective-permute-start(bf16[2,1,640]{2,1,0:T(2,128)(2,1)S(1)} %get-tuple-element.26), channel_id=1, source_target_pairs={{0,1},{1,2},{2,3},{3,0},{4,5},{5,6},{6,7},{7,4},{8,9},{9,10},{10,1... | collective-permute-start | bytes 7688 | tf_op jit(solution)/shard_map/ppermute | solution.py:26
  5.7 6.2 %collective-permute-start.1 = (bf16[2,1,640]{2,1,0:T(2,128)(2,1)S(1)}, bf16[2,1,640]{2,1,0:T(2,128)(2,1)S(1)}, u32[]{:S(2)}, u32[]{:S(2)}) collective-permute-start(bf16[2,1,640]{2,1,0:T(2,128)(2,1)S(1)} %get-tuple-element.27), channel_id=1, source_target_pairs={{1,0},{2,1},{3,2},{0,3},{5,4},{6,5},{7,6},{4,7},{9,8},{10,9},{11,1... | collective-permute-start | bytes 7688 | tf_op jit(solution)/shard_map/ppermute | solution.py:27
  12.9 2.5 %collective-permute-start.2 = (bf16[1,182,640]{2,1,0:T(8,128)(2,1)S(1)}, bf16[1,182,640]{2,1,0:T(8,128)(2,1)S(1)}, u32[]{:S(2)}, u32[]{:S(2)}) collective-permute-start(bf16[1,182,640]{2,1,0:T(8,128)(2,1)S(1)} %get-tuple-element.24), channel_id=1, source_target_pairs={{0,4},{4,8},{8,12},{12,16},{16,20},{20,24},{24,28},{28,32},{32,36}... | collective-permute-start | bytes 698888 | tf_op jit(solution)/shard_map/ppermute | solution.py:26
  15.4 1.3 collective-permute-start.3
  16.8 2.7 %collective-permute-done.2 = bf16[1,182,640]{2,1,0:T(8,128)(2,1)S(1)} collective-permute-done((bf16[1,182,640]{2,1,0:T(8,128)(2,1)S(1)}, bf16[1,182,640]{2,1,0:T(8,128)(2,1)S(1)}, u32[]{:S(2)}, u32[]{:S(2)}) %collective-permute-start.2) | collective-permute-done | bytes 232992 | tf_op jit(solution)/shard_map/ppermute | solution.py:26
  19.5 5.4 %collective-permute-done.3 = bf16[1,182,640]{2,1,0:T(8,128)(2,1)S(1)} collective-permute-done((bf16[1,182,640]{2,1,0:T(8,128)(2,1)S(1)}, bf16[1,182,640]{2,1,0:T(8,128)(2,1)S(1)}, u32[]{:S(2)}, u32[]{:S(2)}) %collective-permute-start.3) | collective-permute-done | bytes 232992 | tf_op jit(solution)/shard_map/ppermute | solution.py:27
  27.1 18.7 %all_to_all.68 = bf16[2,180,640]{1,0,2:T(2,128)(2,1)S(1)} all-to-all(bf16[2,180,640]{1,0,2:T(2,128)(2,1)S(1)} %copy.42), channel_id=1, replica_groups=mesh['lat'=128,'lon'=4] {'lon'}, dimensions={2} | all-to-all | bytes 921600 | tf_op jit(solution)/shard_map/all_to_all | solution.py:154
  46.7 1.5 reshape.31
  48.2 1.8 fusion.12
  51.2 17.0 %all-to-all-start.1 = ((bf16[2,256,2,160]{3,2,0,1:T(2,128)(2,1)}), bf16[2,256,2,160]{3,2,0,1:T(2,128)(2,1)S(1)}, u32[]{:S(2)}, u32[]{:S(2)}) async-start(bf16[2,256,2,160]{3,2,0,1:T(2,128)(2,1)} %copy.45), calls=%async_computation.1 | async-start | bytes 1048576 | tf_op jit(solution)/shard_map/all_to_all | solution.py:159
  68.2 5.8 %legendre.1 = (bf16[2,256,256]{2,1,0:T(8,128)(2,1)}, bf16[2,256,256]{2,1,0:T(8,128)(2,1)}) custom-call(f32[8,256]{1,0:T(8,128)} %constant.9.clone.rows_ref), custom_call_target="tpu_custom_call" | custom-call | tf_op jit(solution)/shard_map/legendre/pallas_call | solution.py:106
  74.1 25.4 %all-to-all-done.1 = bf16[2,256,2,160]{3,2,0,1:T(2,128)(2,1)S(1)} async-done(((bf16[2,256,2,160]{3,2,0,1:T(2,128)(2,1)}), bf16[2,256,2,160]{3,2,0,1:T(2,128)(2,1)S(1)}, u32[]{:S(2)}, u32[]{:S(2)}) %all-to-all-start.1) | async-done | bytes 327712 | tf_op jit(solution)/shard_map/all_to_all | solution.py:159
  100.4 22.8 %all_to_all.69 = bf16[4,256,2,2,160]{1,4,3,2,0:T(8,128)(2,1)S(1)} all-to-all(bf16[4,256,2,2,160]{1,4,3,2,0:T(8,128)(2,1)S(1)} %broadcast_in_dim.2), channel_id=1, replica_groups=mesh['lat'=128,'lon'=4] {'lon'}, dimensions={0} | all-to-all | bytes 2621440 | tf_op jit(solution)/shard_map/all_to_all | solution.py:40
  123.4 1.8 copy.50
  125.3 2.1 %reshape_squeeze.6 = bf16[512,640]{1,0:T(8,128)(2,1)S(1)} reshape(bf16[256,2,1,640]{3,1,0,2:T(2,128)(2,1)} %copy.50) | data formatting | bytes 1310720 | tf_op jit(solution)/shard_map/reshape;squeeze | solution.py:179
  130.9 1.4 fusion.13
  134.4 1.2 fusion.11
  136.0 38.4 %all_to_all.70 = bf16[256,2,2,160]{3,2,1,0:T(2,128)(2,1)S(1)} all-to-all(bf16[256,2,2,160]{3,2,1,0:T(2,128)(2,1)S(1)} %copy.56), channel_id=1, replica_groups=mesh['lat'=128,'lon'=4] {'lat'}, dimensions={0} | all-to-all | bytes 655360 | tf_op jit(solution)/shard_map/all_to_all | solution.py:201
  174.8 1.8 fusion.10
  177.6 16.8 %all_to_all.71 = bf16[2,720,160]{2,0,1:T(2,128)(2,1)S(1)} all-to-all(bf16[2,720,160]{2,0,1:T(2,128)(2,1)S(1)} %copy.59), channel_id=1, replica_groups=mesh['lat'=128,'lon'=4] {'lon'}, dimensions={1} | all-to-all | bytes 921600 | tf_op jit(solution)/shard_map/all_to_all | solution.py:205
  194.7 1.9 reshape.35
  196.6 1.5 multiply_reduce_fusion
  199.4 3.4 %fusion.9 = bf16[360,640]{1,0:T(8,128)(2,1)S(1)} fusion(f32[360,640]{1,0:T(8,128)} %reshape.28, bf16[1280,640]{1,0:T(8,128)(2,1)S(1)} %copy-done, bf16[360,640]{1,0:T(8,128)(2,1)S(1)} %reshape.29, bf16[640,1280]{1,0:T(8,128)(2,1)} %param.15), kind=kOutput, calls=%fused_computation.14 | convolution fusion | flops 1184256000 | bytes 5120000 | tf_op jit(solution)/shard_map/dot_general | solution.py:216
  (60 shorter events, 16.6 us)
Async XLA Ops:
  0.0 199.4 %copy-start = (bf16[1280,640]{1,0:T(8,128)(2,1)S(1)}, bf16[1280,640]{1,0:T(8,128)(2,1)}, u32[]{:S(2)}) copy-start(bf16[1280,640]{1,0:T(8,128)(2,1)} %param.16) | copy-start | bytes 4915204
  0.0 16.7 %copy-start.8 = (f32[3,3,640]{2,1,0:T(4,128)S(1)}, f32[3,3,640]{2,1,0:T(4,128)}, u32[]{:S(2)}) copy-start(f32[3,3,640]{2,1,0:T(4,128)} %param.11) | copy-start | bytes 69124
  1.2 10.7 %collective-permute-start = (bf16[2,1,640]{2,1,0:T(2,128)(2,1)S(1)}, bf16[2,1,640]{2,1,0:T(2,128)(2,1)S(1)}, u32[]{:S(2)}, u32[]{:S(2)}) collective-permute-start(bf16[2,1,640]{2,1,0:T(2,128)(2,1)S(1)} %get-tuple-element.26), channel_id=1, source_target_pairs={{0,1},{1,2},{2,3},{3,0},{4,5},{5,6},{6,7},{7,4},{8,9},{9,10},{10,1... | collective-permute-start | bytes 7688 | tf_op jit(solution)/shard_map/ppermute | solution.py:26
  5.7 7.0 %collective-permute-start.1 = (bf16[2,1,640]{2,1,0:T(2,128)(2,1)S(1)}, bf16[2,1,640]{2,1,0:T(2,128)(2,1)S(1)}, u32[]{:S(2)}, u32[]{:S(2)}) collective-permute-start(bf16[2,1,640]{2,1,0:T(2,128)(2,1)S(1)} %get-tuple-element.27), channel_id=1, source_target_pairs={{1,0},{2,1},{3,2},{0,3},{5,4},{6,5},{7,6},{4,7},{9,8},{10,9},{11,1... | collective-permute-start | bytes 7688 | tf_op jit(solution)/shard_map/ppermute | solution.py:27
  12.8 12.1 %copy-start.2 = (bf16[2,180,640]{2,0,1:T(2,128)(2,1)S(1)}, bf16[2,180,640]{2,0,1:T(2,128)(2,1)}, u32[]{:S(2)}) copy-start(bf16[2,180,640]{2,0,1:T(2,128)(2,1)} %param.10) | copy-start | bytes 1382404
  12.9 6.6 %collective-permute-start.2 = (bf16[1,182,640]{2,1,0:T(8,128)(2,1)S(1)}, bf16[1,182,640]{2,1,0:T(8,128)(2,1)S(1)}, u32[]{:S(2)}, u32[]{:S(2)}) collective-permute-start(bf16[1,182,640]{2,1,0:T(8,128)(2,1)S(1)} %get-tuple-element.24), channel_id=1, source_target_pairs={{0,4},{4,8},{8,12},{12,16},{16,20},{20,24},{24,28},{28,32},{32,36}... | collective-permute-start | bytes 698888 | tf_op jit(solution)/shard_map/ppermute | solution.py:26
  15.4 9.5 %collective-permute-start.3 = (bf16[1,182,640]{2,1,0:T(8,128)(2,1)S(1)}, bf16[1,182,640]{2,1,0:T(8,128)(2,1)S(1)}, u32[]{:S(2)}, u32[]{:S(2)}) collective-permute-start(bf16[1,182,640]{2,1,0:T(8,128)(2,1)S(1)} %get-tuple-element.25), channel_id=1, source_target_pairs={{4,0},{8,4},{12,8},{16,12},{20,16},{24,20},{28,24},{32,28},{36,32}... | collective-permute-start | bytes 698888 | tf_op jit(solution)/shard_map/ppermute | solution.py:27
  26.1 22.1 %copy-start.1 = (bf16[2,180,640]{2,1,0:T(8,128)(2,1)}, bf16[2,180,640]{2,1,0:T(8,128)(2,1)S(1)}, u32[]{:S(2)}) copy-start(bf16[2,180,640]{2,1,0:T(8,128)(2,1)S(1)} %fusion.23) | copy-start | bytes 1382404
  48.2 25.8 %copy-start.5 = (f32[2,256,160]{1,2,0:T(8,128)S(1)}, f32[2,256,160]{1,2,0:T(8,128)}, u32[]{:S(2)}) copy-start(f32[2,256,160]{1,2,0:T(8,128)} %param.12) | copy-start | bytes 983044
  51.2 48.2 %all-to-all-start.1 = ((bf16[2,256,2,160]{3,2,0,1:T(2,128)(2,1)}), bf16[2,256,2,160]{3,2,0,1:T(2,128)(2,1)S(1)}, u32[]{:S(2)}, u32[]{:S(2)}) async-start(bf16[2,256,2,160]{3,2,0,1:T(2,128)(2,1)} %copy.45), calls=%async_computation.1 | async-start | bytes 1048576 | tf_op jit(solution)/shard_map/all_to_all | solution.py:159
  74.0 25.8 %copy-start.6 = (bf16[2,256,256]{2,1,0:T(8,128)(2,1)S(1)}, bf16[2,256,256]{2,1,0:T(8,128)(2,1)}, u32[]{:S(2)}) copy-start(bf16[2,256,256]{2,1,0:T(8,128)(2,1)} %get-tuple-element.7) | copy-start | bytes 786436
  123.4 3.9 %copy-start.3 = (bf16[2,640,160]{1,2,0:T(8,128)(2,1)S(1)}, bf16[2,640,160]{1,2,0:T(8,128)(2,1)}, u32[]{:S(2)}) copy-start(bf16[2,640,160]{1,2,0:T(8,128)(2,1)} %param.13) | copy-start | bytes 1228804
  130.9 2.5 %copy-start.4 = (f32[512,160]{0,1:T(8,128)S(1)}, f32[512,160]{0,1:T(8,128)}, u32[]{:S(2)}) copy-start(f32[512,160]{0,1:T(8,128)} %fusion.46) | copy-start | bytes 983044
  133.4 0.9 copy-start.7
  196.6 2.6 %copy-start.9 = (f32[640]{0:T(1024)S(1)}, f32[640]{0:T(1024)}, u32[]{:S(2)}) copy-start(f32[640]{0:T(1024)} %param.14) | copy-start | bytes 7684

commit v2 on v1

v2 whole, which is shorter than its diff:
```python
import functools
import math

import jax
import jax.numpy as jnp
import numpy as np
from jax import lax
from jax.experimental import pallas as pl
from jax.experimental.pallas import tpu as pltpu
from jax.sharding import PartitionSpec as P

M = 256
norm_eps = 1e-06
underflow_cut = -60.0
edge_rows = 16
bf16 = jnp.bfloat16
f32 = jnp.float32
MESH = pl.DeviceIdType.MESH


def cycle_of_row(rings, depth):
    row = np.arange(rings * depth * 4)
    plane, z = row // depth, row % depth
    return (plane // 4) * (4 * depth) + 4 * z + plane % 4


def latitude_rows(lat_total, rings, depth):
    theta = (cycle_of_row(rings, depth) + 0.5) * (math.pi / lat_total)
    rank = np.arange(1, lat_total + 1)
    rows = np.stack(
        [
            np.cos(theta),
            np.log(np.sin(theta)),
            2.0 * math.pi * math.pi / lat_total * np.sin(theta),
            0.5 * np.log((2.0 * rank + 1.0) / (2.0 * rank)),
        ]
    )
    return np.concatenate([rows, np.zeros_like(rows)]).astype(np.float32)


def fourier_tables(sector, padded, mode_count, rings, depth):
    lon_total = 4 * sector
    z, j, r = np.meshgrid(np.arange(depth), np.arange(2 * rings), np.arange(2), indexing="ij")
    z, j, r = z.ravel(), j.ravel(), r.ravel()
    column = np.arange(4 * padded)
    lon = (column // padded) * sector + column % padded
    inside = (column % padded) < sector
    forward, inverse = [], []
    for core in range(2):
        order = (2 * j + core) * depth + z
        angle = (order[:, None] * lon[None, :] % lon_total) * (2.0 * math.pi / lon_total)
        wave = np.where(r[:, None] == 0, np.cos(angle), -np.sin(angle)) * inside[None, :]
        forward.append(wave / lon_total)
        inverse.append((wave * np.where(order == 0, 1.0, 2.0)[:, None]).T)
    forward = np.stack(forward).astype(np.float32).astype(bf16)
    inverse = np.concatenate(inverse, axis=1).reshape(4, padded, mode_count * 2)
    return jnp.asarray(forward), jnp.asarray(inverse.astype(np.float32).astype(bf16))


def legendre_fill(order, rows_ref, raise_ref, lower_ref, table_ref):
    degrees, width = table_ref.shape
    order_float = order.astype(f32)
    cosine = rows_ref[0:1, :]
    log_sine = rows_ref[1:2, :]
    rank = lax.broadcasted_iota(jnp.int32, (1, width), 1) + 1
    log_norm = jnp.sum(jnp.where(rank <= order, rows_ref[3:4, :], 0.0), axis=1, keepdims=True)
    log_start = -0.5 * math.log(4.0 * math.pi) + log_norm + order_float * log_sine
    start = jnp.where(log_start > underflow_cut, jnp.exp(jnp.maximum(log_start, underflow_cut)), 0.0)
    degree = lax.broadcasted_iota(jnp.int32, (degrees, width), 0).astype(f32)
    raise_coef = jnp.sqrt(
        jnp.maximum(4.0 * degree * degree - 1.0, 0.0)
        / jnp.maximum(degree * degree - order_float * order_float, 1.0)
    )
    below = degree - 1.0
    lower_coef = jnp.sqrt(
        jnp.maximum(below * below - order_float * order_float, 0.0)
        / jnp.maximum(4.0 * below * below - 1.0, 1.0)
    )
    raise_ref[...] = raise_coef * cosine
    lower_ref[...] = raise_coef * lower_coef

    def advance(degree_now, carried):
        previous, earlier = carried
        row = pl.ds(degree_now, 1)
        recurred = raise_ref[row, :] * previous - lower_ref[row, :] * earlier
        current = jnp.where(degree_now == order, start, recurred)
        table_ref[row, :] = current
        return current, previous

    blank = 0.0 * raise_ref[0:1, :]
    lax.fori_loop(0, degrees, advance, (blank, blank), unroll=8)


def block_kernel(
    rings,
    depth,
    spans,
    grid_hbm,
    conv_ref,
    gain_hbm,
    mix_hbm,
    norm_ref,
    expand_hbm,
    reduce_hbm,
    forward_hbm,
    inverse_hbm,
    rows_ref,
    out_ref,
    grid_v,
    halo_v,
    edge_out,
    edge_in,
    wide_v,
    first_v,
    circle_v,
    modes_v,
    column_v,
    turned_v,
    meridian_v,
    coef_own,
    coef_out,
    coef_in,
    gain_part,
    gain_all,
    gain_v,
    mix_v,
    gained_v,
    mixed_out,
    mixed_v,
    cycle_v,
    back_v,
    column_back,
    modes_all,
    spectral_own,
    spectral_out,
    spectral_in,
    normed_v,
    total_v,
    expand_v,
    reduce_v,
    forward_v,
    inverse_v,
    swap_v,
    raise_v,
    lower_v,
    table_v,
    analysis_v,
    synthesis_v,
    sems,
    local_sems,
):
    sector, channels = grid_v.shape[1:]
    padded = first_v.shape[1]
    lat_count = rings * depth * 2
    swap_rows = 4 * rings
    share = mix_hbm.shape[1]
    half = coef_own.shape[0]
    lat = lax.axis_index("lat")
    lon = lax.axis_index("lon")
    x_high = lat % 2
    z = (lat // 2) % depth
    y = lat // (2 * depth)
    x_low = lon // 2
    core = lon % 2
    plane = 4 * y + 2 * x_high + x_low
    slot = (2 * y + x_high) * 2 + core
    order = plane * depth + z
    twin = lon + 1 - 2 * core
    across = (lon + 2) % 4
    opposite = 3 - lon
    lat_up = (lat + 1) % lat_count
    lat_down = (lat + lat_count - 1) % lat_count
    lat_pair = lat + 1 - 2 * x_high
    lon_up = (lon + 1) % 4
    lon_down = (lon + 3) % 4
    diagonal = core == x_low

    names = {}

    def sem(name):
        index = names.setdefault(name, len(names))
        assert index < sems.shape[0], "semaphores"
        return sems.at[index]

    def send(source, target, name, lat_to, lon_to):
        copy = pltpu.make_async_remote_copy(
            src_ref=source,
            dst_ref=target,
            send_sem=sem(name + ".s"),
            recv_sem=sem(name + ".r"),
            device_id={"lat": lat_to, "lon": lon_to},
            device_id_type=MESH,
        )
        copy.start()

    def wait(ref, semaphore):
        pltpu.make_async_copy(ref, ref, semaphore).wait()

    def arrived(ref, name):
        wait(ref, sem(name + ".r"))

    def left(ref, name):
        wait(ref, sem(name + ".s"))

    def z_offset(i):
        return depth // 2 + (1 - 2 * (i % 2)) * ((i + 1) // 2)

    def ring_peer(i):
        return (z + z_offset(i)) % depth

    def lat_of(y_to, z_to, high_to):
        return (y_to * depth + z_to) * 2 + high_to

    def order_peer(i):
        return lat_of(i // 4, z, (i // 2) % 2), 2 * core + i % 2

    def cycle_peer(i):
        return lat_of(i // 4, z, (i % 4) // 2), 2 * (i % 2) + x_low

    barrier = pltpu.get_barrier_semaphore()

    def greet(lat_to, lon_to):
        pl.semaphore_signal(
            barrier, inc=1, device_id={"lat": lat_to, "lon": lon_to}, device_id_type=MESH
        )

    for lat_to in (lat_up, lat_down):
        for lon_to in (lon, lon_up, lon_down):
            greet(lat_to, lon_to)
    greet(lat, lon_up)
    greet(lat, lon_down)
    greet(lat, across)
    greet(lat_pair, across)
    greet(lat_pair, opposite)

    @pl.loop(0, depth - 1)
    def _(i):
        greet(lat_of(y, ring_peer(i), x_high), lon)

    @pl.loop(0, swap_rows)
    def _(i):
        for peer in (order_peer, cycle_peer):
            lat_to, lon_to = peer(i)

            @pl.when(jnp.logical_or(lat_to != lat, lon_to != lon))
            def _():
                greet(lat_to, lon_to)

    loads = {}

    def load(name, source, target):
        copy = pltpu.make_async_copy(source, target, local_sems.at[len(loads)])
        copy.start()
        loads[name] = copy

    load("grid", grid_hbm, grid_v)
    mix_own = mix_v.at[:, pl.ds(pl.multiple_of(lon * share, 16), share), :]
    load("mix", mix_hbm, mix_own)
    load("gain0", gain_hbm.at[:, :, pl.ds(0, half)], gain_part.at[0])
    load("gain1", gain_hbm.at[:, :, pl.ds(half, half)], gain_part.at[1])
    load("forward", forward_hbm.at[core], forward_v)
    load("inverse0", inverse_hbm.at[lon], inverse_v.at[0])
    load("inverse1", inverse_hbm.at[across], inverse_v.at[1])
    load("expand", expand_hbm, expand_v)
    load("reduce", reduce_hbm, reduce_v)

    loads["grid"].wait()
    for t in range(2):
        edge_out[0, t] = grid_v[t, 0:edge_rows, :]
        edge_out[1, t] = grid_v[t, sector - edge_rows : sector, :]
    pl.semaphore_wait(barrier, 11 + depth - 1 + 2 * swap_rows - 2 * diagonal.astype(jnp.int32))

    for side, lon_to in ((0, lon_down), (1, lon_up)):
        send(edge_out.at[side, 1], edge_in.at[side, 0], "edge", lat_up, lon_to)
        send(edge_out.at[side, 0], edge_in.at[side, 3], "edge", lat_down, lon_to)
        send(edge_out.at[side], edge_in.at[side, pl.ds(1, 2)], "edge", lat, lon_to)
    for k, (base, width) in enumerate(spans):
        lanes = pl.ds(base, width)
        send(grid_v.at[1, :, lanes], halo_v.at[0, :, lanes], f"halo{k}", lat_up, lon)
        send(grid_v.at[0, :, lanes], halo_v.at[1, :, lanes], f"halo{k}", lat_down, lon)

    loads["mix"].wait()
    loads["gain0"].wait()
    loads["gain1"].wait()
    send(mix_own, mix_own, "mixx", lat_pair, across)
    send(mix_own, mix_own, "mixc", lat, twin)
    gain_all[lon] = gain_part[core]
    send(gain_part.at[core], gain_all.at[lon], "gain", lat_pair, across)
    send(gain_part.at[1 - core], gain_all.at[lon], "gain", lat_pair, opposite)
    send(gain_part.at[1 - core], gain_all.at[lon], "gain", lat, twin)

    side = swap_rows * depth
    row = lax.broadcasted_iota(jnp.int32, (side, side), 0)
    column = lax.broadcasted_iota(jnp.int32, (side, side), 1)
    first_v[:, padded - 16 : padded, :] = jnp.zeros((2, 16, channels), bf16)
    swap_v[0] = (column == (row % depth) * swap_rows + row // depth).astype(f32).astype(bf16)
    swap_v[1] = (column == (row % swap_rows) * depth + row // swap_rows).astype(f32).astype(bf16)
    legendre_fill(order, rows_ref, raise_v, lower_v, table_v)
    table = table_v[...]
    analysis_v[...] = (table * rows_ref[2:3, :]).astype(bf16).reshape(analysis_v.shape)
    synthesis_v[...] = table.T.astype(bf16)

    above = (lat > 0).astype(f32)
    below = (lat < lat_count - 1).astype(f32)
    scales = (above, None, None, below)

    def stage_conv(k):
        base, width = spans[k]
        lanes = pl.ds(base, width)
        if k == 0:
            arrived(edge_in, "edge")
        arrived(halo_v.at[:, :, lanes], f"halo{k}")
        for line in range(4):
            source = (halo_v.at[0], grid_v.at[0], grid_v.at[1], halo_v.at[1])[line]
            body = source[:, lanes].astype(f32)
            before = edge_in[1, line, :, lanes].astype(f32)[edge_rows - 1 :]
            after = edge_in[0, line, :, lanes].astype(f32)[:1]
            if scales[line] is not None:
                body, before, after = (scales[line] * v for v in (body, before, after))
            wide_v[line, 8 : 8 + sector, lanes] = body
            wide_v[line, 7:8, lanes] = before
            wide_v[line, 8 + sector : 9 + sector, lanes] = after
        for t in range(2):
            filtered = None
            for i in range(3):
                for j in range(3):
                    term = conv_ref[i, j : j + 1, lanes] * wide_v[t + i, 7 + j : 7 + j + sector, lanes]
                    filtered = term if filtered is None else filtered + term
            centre = wide_v[t + 1, 8 : 8 + sector, lanes]
            first_v[t, 0:sector, lanes] = (centre + jax.nn.gelu(filtered)).astype(bf16)
        send(first_v.at[1 - x_low, :, lanes], circle_v.at[lon, :, lanes], f"lonx{k}", lat, across)
        send(first_v.at[x_low, :, lanes], circle_v.at[lon, :, lanes], f"lonc{k}", lat, twin)
        circle_v[lon, :, lanes] = first_v[x_low, :, lanes]

    def stage_relay(k):
        base, width = spans[k]
        lanes = pl.ds(base, width)
        arrived(circle_v.at[across, :, lanes], f"lonx{k}")
        send(circle_v.at[across, :, lanes], circle_v.at[across, :, lanes], f"lonr{k}", lat, twin)

    def stage_fourier(k):
        base, width = spans[k]
        lanes = pl.ds(base, width)
        if k == 0:
            loads["forward"].wait()
        arrived(circle_v.at[twin, :, lanes], f"lonc{k}")
        arrived(circle_v.at[opposite, :, lanes], f"lonr{k}")
        circle = circle_v[:, :, lanes].reshape(4 * padded, width)
        modes = jnp.dot(forward_v[...], circle, preferred_element_type=f32).astype(bf16)
        modes_v[:, :, lanes] = modes.reshape(depth, swap_rows, width)

        @pl.loop(0, depth - 1)
        def _(i):
            z_to = ring_peer(i)
            send(
                modes_v.at[z_to, :, lanes],
                column_v.at[z, :, lanes],
                f"ring{k}",
                lat_of(y, z_to, x_high),
                lon,
            )

        column_v[z, :, lanes] = modes_v[z, :, lanes]

    def stage_turn(k):
        base, width = spans[k]
        lanes = pl.ds(base, width)
        arrived(column_v.at[pl.ds(0, depth - 1), :, lanes], f"ring{k}")
        column = column_v[:, :, lanes].reshape(side, width)
        turned = jnp.dot(swap_v[0], column, preferred_element_type=f32).astype(bf16)
        turned_v[:, :, lanes] = turned.reshape(swap_rows, depth, width)

        @pl.loop(0, swap_rows)
        def _(i):
            to = (slot + i) % swap_rows
            lat_to, lon_to = order_peer(to)

            @pl.when(jnp.logical_or(lat_to != lat, lon_to != lon))
            def _():
                send(
                    turned_v.at[to, :, lanes],
                    meridian_v.at[plane, :, lanes],
                    f"plane{k}",
                    lat_to,
                    lon_to,
                )

        @pl.when(diagonal)
        def _():
            meridian_v[plane, :, lanes] = turned_v[slot, :, lanes]

    def count_wait(ref, lanes, semaphore):
        @pl.when(diagonal)
        def _():
            wait(ref.at[pl.ds(0, swap_rows - 1), :, lanes], semaphore)

        @pl.when(jnp.logical_not(diagonal))
        def _():
            wait(ref.at[:, :, lanes], semaphore)

    def stage_analysis(k):
        base, width = spans[k]
        lanes = pl.ds(base, width)
        count_wait(meridian_v, lanes, sem(f"plane{k}.r"))
        meridian = meridian_v[:, :, lanes].reshape(side, width)
        coef_out[:, lanes] = jnp.dot(analysis_v[1 - core], meridian, preferred_element_type=f32)
        send(coef_out.at[:, lanes], coef_in.at[:, lanes], f"coef{k}", lat, twin)
        coef_own[:, lanes] = jnp.dot(analysis_v[core], meridian, preferred_element_type=f32)

    def stage_gain(k):
        base, width = spans[k]
        lanes = pl.ds(base, width)
        if k == 0:
            arrived(gain_all.at[pl.ds(0, 3)], "gain")
            for r in range(2):
                whole = gain_all[:, r].reshape(channels, half)
                gain_v[r] = whole.T
            arrived(mix_v.at[:, pl.ds(0, share), :], "mixx")
            opposite_mix = mix_v.at[:, pl.ds(pl.multiple_of(across * share, 16), share), :]
            send(opposite_mix, opposite_mix, "mixr", lat, twin)
        arrived(coef_in.at[:, lanes], f"coef{k}")
        own = coef_own[:, lanes]
        other = coef_in[:, lanes]
        real = jnp.where(core == 0, own, other)
        imag = jnp.where(core == 0, other, own)
        gain_real = gain_v[0, :, lanes]
        gain_imag = gain_v[1, :, lanes]
        gained_v[0:half, lanes] = (gain_real * real - gain_imag * imag).astype(bf16)
        gained_v[half : 2 * half, lanes] = (gain_real * imag + gain_imag * real).astype(bf16)

    def stage_mix(k):
        base, width = spans[k]
        lanes = pl.ds(base, width)
        if k == 0:
            arrived(mix_v.at[:, pl.ds(0, share), :], "mixc")
            arrived(mix_v.at[:, pl.ds(0, share), :], "mixr")
        gained = gained_v[...]
        contract = (((1,), (1,)), ((), ()))
        by_real = lax.dot_general(gained, mix_v[0, lanes, :], contract, preferred_element_type=f32)
        by_imag = lax.dot_general(gained, mix_v[1, lanes, :], contract, preferred_element_type=f32)
        real = by_real[:half] - by_imag[half:]
        imag = by_imag[:half] + by_real[half:]
        mixed_out[:, lanes] = jnp.where(core == 0, imag, real).astype(bf16)
        send(mixed_out.at[:, lanes], mixed_v.at[core, :, lanes], f"mixed{k}", lat, twin)
        mixed_v[core, :, lanes] = jnp.where(core == 0, real, imag).astype(bf16)

    def stage_synthesis(k):
        base, width = spans[k]
        lanes = pl.ds(base, width)
        arrived(mixed_v.at[1 - core, :, lanes], f"mixed{k}")
        mixed = mixed_v[:, :, lanes].reshape(2 * half, width)
        cycle = jnp.dot(synthesis_v[...], mixed, preferred_element_type=f32).astype(bf16)
        cycle_v[:, :, lanes] = cycle.reshape(swap_rows, depth, width)

        @pl.loop(0, swap_rows)
        def _(i):
            to = (plane + i) % swap_rows
            lat_to, lon_to = cycle_peer(to)

            @pl.when(jnp.logical_or(lat_to != lat, lon_to != lon))
            def _():
                send(
                    cycle_v.at[to, :, lanes],
                    back_v.at[slot, :, lanes],
                    f"plback{k}",
                    lat_to,
                    lon_to,
                )

        @pl.when(diagonal)
        def _():
            back_v[slot, :, lanes] = cycle_v[plane, :, lanes]

    def stage_turn_back(k):
        base, width = spans[k]
        lanes = pl.ds(base, width)
        count_wait(back_v, lanes, sem(f"plback{k}.r"))
        back = back_v[:, :, lanes].reshape(side, width)
        turned = jnp.dot(swap_v[1], back, preferred_element_type=f32).astype(bf16)
        column_back[:, :, lanes] = turned.reshape(depth, swap_rows, width)

        @pl.loop(0, depth - 1)
        def _(i):
            z_to = ring_peer(i)
            send(
                column_back.at[z_to, :, lanes],
                modes_all.at[core, z, :, lanes],
                f"rgback{k}",
                lat_of(y, z_to, x_high),
                lon,
            )

        modes_all[core, z, :, lanes] = column_back[z, :, lanes]

    def stage_share(k):
        base, width = spans[k]
        lanes = pl.ds(base, width)
        arrived(modes_all.at[core, pl.ds(0, depth - 1), :, lanes], f"rgback{k}")
        send(modes_all.at[core, :, :, lanes], modes_all.at[core, :, :, lanes], f"modes{k}", lat, twin)

    def stage_inverse(k):
        base, width = spans[k]
        lanes = pl.ds(base, width)
        if k == 0:
            loads["inverse0"].wait()
            loads["inverse1"].wait()
        arrived(modes_all.at[1 - core, :, :, lanes], f"modes{k}")
        modes = modes_all[:, :, :, lanes].reshape(2 * side, width)
        spectral_out[:, lanes] = jnp.dot(
            inverse_v[1], modes, preferred_element_type=f32
        ).astype(bf16)
        send(spectral_out.at[:, lanes], spectral_in.at[:, lanes], f"spec{k}", lat, across)
        spectral_own[:, lanes] = jnp.dot(inverse_v[0], modes, preferred_element_type=f32)

    def finish(which, spectral):
        second = (first_v[which].astype(f32) + spectral).astype(bf16).astype(f32)
        scale = lax.rsqrt(jnp.mean(second * second, axis=-1, keepdims=True) + norm_eps)
        normed_v[...] = (second * norm_ref[...] * scale).astype(bf16)
        total_v[...] = second
        hidden_width = expand_v.shape[1]
        step = min(256, hidden_width)
        for base in range(0, hidden_width, step):
            columns = slice(base, base + step)
            hidden = jax.nn.gelu(
                jnp.dot(normed_v[...], expand_v[:, columns], preferred_element_type=f32)
            ).astype(bf16)
            total_v[...] += jnp.dot(hidden, reduce_v[columns, :], preferred_element_type=f32)
        out_ref[which] = total_v[0:sector, :].astype(bf16)

    def pipeline(stages):
        count = len(spans)
        for beat in range(count + len(stages) - 1):
            for depth_now, stage in enumerate(stages):
                k = beat - depth_now
                if 0 <= k < count:
                    stage(k)

    pipeline([stage_conv, stage_relay, stage_fourier, stage_turn, stage_analysis, stage_gain])
    pipeline([stage_mix, stage_synthesis, stage_turn_back, stage_share, stage_inverse])

    loads["expand"].wait()
    loads["reduce"].wait()
    finish(x_low, spectral_own[...])
    for k, (base, width) in enumerate(spans):
        arrived(spectral_in.at[:, pl.ds(base, width)], f"spec{k}")
    finish(1 - x_low, spectral_in[...].astype(f32))

    left(edge_in, "edge")
    left(mix_v.at[:, pl.ds(0, share), :], "mixx")
    left(mix_v.at[:, pl.ds(0, share), :], "mixc")
    left(mix_v.at[:, pl.ds(0, share), :], "mixr")
    left(gain_all.at[pl.ds(0, 3)], "gain")
    for k, (base, width) in enumerate(spans):
        lanes = pl.ds(base, width)
        left(halo_v.at[:, :, lanes], f"halo{k}")
        for name in ("lonx", "lonc", "lonr"):
            left(circle_v.at[0, :, lanes], f"{name}{k}")
        left(column_v.at[pl.ds(0, depth - 1), :, lanes], f"ring{k}")
        count_wait(meridian_v, lanes, sem(f"plane{k}.s"))
        left(coef_in.at[:, lanes], f"coef{k}")
        left(mixed_out.at[:, lanes], f"mixed{k}")
        count_wait(back_v, lanes, sem(f"plback{k}.s"))
        left(column_v.at[pl.ds(0, depth - 1), :, lanes], f"rgback{k}")
        left(modes_all.at[0, :, :, lanes], f"modes{k}")
        left(spectral_out.at[:, lanes], f"spec{k}")


def spans_of(channels, pieces):
    tiles = channels // 128
    cuts = [tiles * i // pieces for i in range(pieces + 1)]
    return [(128 * a, 128 * (b - a)) for a, b in zip(cuts, cuts[1:])]


chunk_count = 1


def shards(
    rings,
    depth,
    grid_state,
    conv_weight,
    spectral_gain,
    spectral_weight,
    norm_gain,
    expand_weight,
    reduce_weight,
):
    two, sector, channels = grid_state.shape
    padded = -(-sector // 16) * 16
    degrees = spectral_gain.shape[1]
    lat_total = 4 * rings * depth
    side = lat_total
    swap_rows = 4 * rings
    half = degrees // 2
    share = channels // 4
    hidden_width = expand_weight.shape[1]
    spans = spans_of(channels, chunk_count)
    forward, inverse = fourier_tables(sector, padded, degrees, rings, depth)
    rows = jnp.asarray(latitude_rows(lat_total, rings, depth))
    anywhere = pl.BlockSpec(memory_space=pl.ANY)
    vmem = pl.BlockSpec(memory_space=pltpu.VMEM)
    scratch = [
        ((2, sector, channels), bf16),
        ((2, sector, channels), bf16),
        ((2, 2, edge_rows, channels), bf16),
        ((2, 4, edge_rows, channels), bf16),
        ((4, -(-(sector + 16) // 8) * 8, channels), f32),
        ((2, padded, channels), bf16),
        ((4, padded, channels), bf16),
        ((depth, swap_rows, channels), bf16),
        ((depth, swap_rows, channels), bf16),
        ((swap_rows, depth, channels), bf16),
        ((swap_rows, depth, channels), bf16),
        ((half, channels), f32),
        ((half, channels), f32),
        ((half, channels), f32),
        ((2, 2, share, half), f32),
        ((4, 2, share, half), f32),
        ((2, half, channels), f32),
        ((2, channels, channels), bf16),
        ((2 * half, channels), bf16),
        ((half, channels), bf16),
        ((2, half, channels), bf16),
        ((swap_rows, depth, channels), bf16),
        ((swap_rows, depth, channels), bf16),
        ((depth, swap_rows, channels), bf16),
        ((2, depth, swap_rows, channels), bf16),
        ((padded, channels), f32),
        ((padded, channels), bf16),
        ((padded, channels), bf16),
        ((padded, channels), bf16),
        ((padded, channels), f32),
        ((channels, hidden_width), bf16),
        ((hidden_width, channels), bf16),
        ((side, 4 * padded), bf16),
        ((2, padded, 2 * side), bf16),
        ((2, side, side), bf16),
        ((degrees, lat_total), f32),
        ((degrees, lat_total), f32),
        ((degrees, lat_total), f32),
        ((2, half, lat_total), bf16),
        ((lat_total, degrees), bf16),
    ]
    return pl.pallas_call(
        functools.partial(block_kernel, rings, depth, spans),
        out_shape=jax.ShapeDtypeStruct(grid_state.shape, bf16),
        in_specs=[anywhere, vmem, anywhere, anywhere, vmem] + [anywhere] * 4 + [vmem],
        out_specs=vmem,
        scratch_shapes=[pltpu.VMEM(*s) for s in scratch]
        + [
            pltpu.SemaphoreType.DMA((10 + 24 * len(spans),)),
            pltpu.SemaphoreType.DMA((9,)),
        ],
        compiler_params=pltpu.CompilerParams(
            collective_id=0, has_side_effects=True, vmem_limit_bytes=60 * 1024 * 1024
        ),
        name="block_pair",
    )(
        grid_state,
        conv_weight,
        jnp.swapaxes(spectral_gain, 1, 2),
        jnp.swapaxes(spectral_weight, 1, 2),
        norm_gain.reshape(1, channels),
        expand_weight,
        reduce_weight,
        forward,
        inverse,
        rows,
    )


def solution(mesh):
    lat_count = mesh.shape["lat"]
    rings = max(1, lat_count // 32)
    depth = lat_count // (2 * rings)
    return jax.shard_map(
        functools.partial(shards, rings, depth),
        mesh=mesh,
        in_specs=(
            P("lat", "lon", None),
            P(),
            P(None, None, "lon"),
            P(None, None, "lon"),
            P(),
            P(),
            P(),
        ),
        out_specs=P("lat", "lon", None),
        check_vma=False,
    )
```

time: 205 us -> 112 us (0.55)
  Pallas kernels: 5.8 us -> 106 us
  blocking collectives: 96.7 us -> 0 us
  waiting for transfers between devices: 34.3 us -> 0 us
  starting transfers between devices: 31.4 us -> 0 us
  local copies, waits for them, and re-layouts: 19.9 us -> 5.25 us
  matrix products: 12.5 us -> 0 us
  other arithmetic: 3.16 us -> 0 us
    pallas_call x1, Pallas kernels: 5.8 us -> 106 us  [shards(): pl.pallas_call(functools.partial(block_kernel, rings, depth, spans), out_...]
    all_to_all x4 -> x0, blocking collectives: 96.7 us -> none  [the longest x1 38.4 us: shards(): lax.all_to_all(cycle_modes, 'lat', split_axis=0, concat_axis=1, tiled=True)]
    all_to_all x1 -> x0, waiting for transfers between devices: 25.4 us -> none  [shards(): lax.all_to_all(spectrum, 'lat', split_axis=1, concat_axis=0, tiled=True)]
    all_to_all x1 -> x0, starting transfers between devices: 17 us -> none  [shards(): lax.all_to_all(spectrum, 'lat', split_axis=1, concat_axis=0, tiled=True)]
    ppermute x4 -> x0, starting transfers between devices: 14.4 us -> none  [the longest x2 7.46 us: padded_2(): after = lax.ppermute(initial, axis, down)]
    dot_general x9 -> x0, matrix products: 12.5 us -> none  [the longest x1 3.42 us: shards(): update = jnp.dot(hidden, reduce_weight, preferred_element_type=jnp.float32)]
    ppermute x4 -> x0, waiting for transfers between devices: 8.88 us -> none  [the longest x2 6.14 us: padded_2(): after = lax.ppermute(initial, axis, down)]
    convert_element_type x6 -> x0, local copies, waits for them, and re-layouts: 5.79 us -> none  [the longest x2 2.22 us: shards(): spectral_out = lax.all_to_all(all_lons.astype(jnp.bfloat16), 'lon', split...]
  transfers between devices with their start and end apart: 5 -> 0, of which waited for: 4 -> 0; matrix products, arithmetic and copies ran while one was open for 0% -> 0% of each run, Pallas kernels for 3% -> 0%
where the time goes in v2:
time: 112 us; the launch traced here: 111 us
  Pallas kernels  106 us (95%)
  local copies, waits for them, and re-layouts  5.25 us (5%)
    pallas_call x1, Pallas kernels, shards(): pl.pallas_call(functools.partial(block_kernel, rings, depth, spans), out_...  106 us

profile of v2, /device:TPU:1, one launch (start us, length us, event | category | flops | bytes accessed | tf_op | source)
XLA Modules:
  0.0 111.4 jit_solution(12433532456918163987)
XLA Ops:
  0.0 1.3 %reshape.3.norm_ref = f32[1,640]{1,0:T(1,128)} reshape(f32[640]{0:T(1024)} %param.14) | data formatting | bytes 5120 | tf_op jit(solution)/shard_map/reshape | solution.py:663
  1.3 1.8 %copy.11.grid_hbm = bf16[2,180,640]{2,1,0:T(8,128)(2,1)} copy(bf16[2,180,640]{2,0,1:T(2,128)(2,1)} %param.10) | data formatting | bytes 921600 | tf_op args[0]
  3.1 106.1 %block_pair.1 = bf16[2,180,640]{2,1,0:T(8,128)(2,1)} custom-call(bf16[2,180,640]{2,1,0:T(8,128)(2,1)} %copy.11.grid_hbm, f32[3,3,640]{2,1,0:T(4,128)} %conv_ref.1, f32[2,160,256]{2,1,0:T(8,128)} %bitcast.3, bf16[2,160,640]{2,1,0:T(8,128)(2,1)} %bitcast.2, f32[1,640]{1,0:T(1,128)} %reshape.3.norm_ref, bf16[640,1280]{1,0:T(8,128)(2,1)} %expand_hbm.1, ...), custom_call_target="tpu_custom_call" | custom-call | tf_op jit(solution)/shard_map/block_pair/pallas_call | solution.py:644
  109.2 2.1 %copy.12 = bf16[2,180,640]{2,0,1:T(2,128)(2,1)} copy(bf16[2,180,640]{2,1,0:T(8,128)(2,1)} %block_pair.1) | data formatting | bytes 921600 | tf_op jit(solution)/shard_map/block_pair/pallas_call | solution.py:644

commit v3 on v2

--- a/solution.py
+++ b/solution.py
@@ -95,15 +95,20 @@
     rings,
     depth,
     spans,
+    spans_back,
     grid_hbm,
-    conv_ref,
+    conv_hbm,
     gain_hbm,
     mix_hbm,
-    norm_ref,
+    norm_hbm,
     expand_hbm,
     reduce_hbm,
     forward_hbm,
     inverse_hbm,
+    rows_hbm,
+    out_hbm,
+    conv_ref,
+    norm_ref,
     rows_ref,
     out_ref,
     grid_v,
@@ -254,6 +259,9 @@
         loads[name] = copy
 
     load("grid", grid_hbm, grid_v)
+    load("rows", rows_hbm, rows_ref)
+    load("conv", conv_hbm, conv_ref)
+    load("norm", norm_hbm, norm_ref)
     mix_own = mix_v.at[:, pl.ds(pl.multiple_of(lon * share, 16), share), :]
     load("mix", mix_hbm, mix_own)
     load("gain0", gain_hbm.at[:, :, pl.ds(0, half)], gain_part.at[0])
@@ -265,29 +273,27 @@
     load("reduce", reduce_hbm, reduce_v)
 
     loads["grid"].wait()
-    for t in range(2):
-        edge_out[0, t] = grid_v[t, 0:edge_rows, :]
-        edge_out[1, t] = grid_v[t, sector - edge_rows : sector, :]
+    blank = jnp.zeros((8 - channels // 128, 128), f32)
+    for side, at in ((0, 0), (1, sector - 8)):
+        pieces = []
+        for t in range(2):
+            line = grid_v[t, at : at + 8, :].astype(f32)[7 * side : 7 * side + 1]
+            pieces += [line[:, base : base + 128] for base in range(0, channels, 128)] + [blank]
+        edge_out[side] = jnp.concatenate(pieces, axis=0).astype(bf16)
     pl.semaphore_wait(barrier, 11 + depth - 1 + 2 * swap_rows - 2 * diagonal.astype(jnp.int32))
 
     for side, lon_to in ((0, lon_down), (1, lon_up)):
-        send(edge_out.at[side, 1], edge_in.at[side, 0], "edge", lat_up, lon_to)
-        send(edge_out.at[side, 0], edge_in.at[side, 3], "edge", lat_down, lon_to)
-        send(edge_out.at[side], edge_in.at[side, pl.ds(1, 2)], "edge", lat, lon_to)
-    for k, (base, width) in enumerate(spans):
+        for source, lat_to in ((0, lat_up), (1, lat), (2, lat_down)):
+            send(edge_out.at[side], edge_in.at[side, source], "edge", lat_to, lon_to)
+    def stage_halo(k):
+        base, width = spans[k]
         lanes = pl.ds(base, width)
         send(grid_v.at[1, :, lanes], halo_v.at[0, :, lanes], f"halo{k}", lat_up, lon)
         send(grid_v.at[0, :, lanes], halo_v.at[1, :, lanes], f"halo{k}", lat_down, lon)
 
-    loads["mix"].wait()
-    loads["gain0"].wait()
-    loads["gain1"].wait()
-    send(mix_own, mix_own, "mixx", lat_pair, across)
-    send(mix_own, mix_own, "mixc", lat, twin)
-    gain_all[lon] = gain_part[core]
-    send(gain_part.at[core], gain_all.at[lon], "gain", lat_pair, across)
-    send(gain_part.at[1 - core], gain_all.at[lon], "gain", lat_pair, opposite)
-    send(gain_part.at[1 - core], gain_all.at[lon], "gain", lat, twin)
+    ahead = min(halo_ahead, len(spans))
+    for k in range(ahead):
+        stage_halo(k)
 
     side = swap_rows * depth
     row = lax.broadcasted_iota(jnp.int32, (side, side), 0)
@@ -295,6 +301,9 @@
     first_v[:, padded - 16 : padded, :] = jnp.zeros((2, 16, channels), bf16)
     swap_v[0] = (column == (row % depth) * swap_rows + row // depth).astype(f32).astype(bf16)
     swap_v[1] = (column == (row % swap_rows) * depth + row // swap_rows).astype(f32).astype(bf16)
+    loads["rows"].wait()
+    loads["conv"].wait()
+    loads["norm"].wait()
     legendre_fill(order, rows_ref, raise_v, lower_v, table_v)
     table = table_v[...]
     analysis_v[...] = (table * rows_ref[2:3, :]).astype(bf16).reshape(analysis_v.shape)
@@ -303,6 +312,11 @@
     above = (lat > 0).astype(f32)
     below = (lat < lat_count - 1).astype(f32)
     scales = (above, None, None, below)
+
+    def edge_line(side, line, base, width):
+        block = edge_in[side, (line + 1) // 2].astype(f32)
+        row = 8 * (1 - line % 2) + base // 128
+        return jnp.concatenate([block[i : i + 1] for i in range(row, row + width // 128)], axis=1)
 
     def stage_conv(k):
         base, width = spans[k]
@@ -313,8 +327,7 @@
         for line in range(4):
             source = (halo_v.at[0], grid_v.at[0], grid_v.at[1], halo_v.at[1])[line]
             body = source[:, lanes].astype(f32)
-            before = edge_in[1, line, :, lanes].astype(f32)[edge_rows - 1 :]
-            after = edge_in[0, line, :, lanes].astype(f32)[:1]
+            after, before = (edge_line(side, line, base, width) for side in range(2))
             if scales[line] is not None:
                 body, before, after = (scales[line] * v for v in (body, before, after))
             wide_v[line, 8 : 8 + sector, lanes] = body
@@ -331,6 +344,22 @@
         send(first_v.at[1 - x_low, :, lanes], circle_v.at[lon, :, lanes], f"lonx{k}", lat, across)
         send(first_v.at[x_low, :, lanes], circle_v.at[lon, :, lanes], f"lonc{k}", lat, twin)
         circle_v[lon, :, lanes] = first_v[x_low, :, lanes]
+        if k + ahead < len(spans):
+            stage_halo(k + ahead)
+
+    def send_weights():
+        loads["mix"].wait()
+        loads["gain0"].wait()
+        loads["gain1"].wait()
+        gain_all[lon] = gain_part[core]
+        rows = pl.ds(pl.multiple_of(lon * share, 16), share)
+        for i, lat_to in ((0, lat_pair), (1, lat)):
+            part = mix_v.at[i, rows, :]
+            send(part, part, "mixx", lat_to, across)
+            send(gain_part.at[core, i], gain_all.at[lon, i], "gain", lat_to, across)
+            send(gain_part.at[1 - core, i], gain_all.at[lon, i], "gain", lat_to, opposite)
+        send(mix_own, mix_own, "mixc", lat, twin)
+        send(gain_part.at[1 - core], gain_all.at[lon], "gain", lat, twin)
 
     def stage_relay(k):
         base, width = spans[k]
@@ -401,6 +430,10 @@
     def stage_analysis(k):
         base, width = spans[k]
         lanes = pl.ds(base, width)
+        if k == 0:
+            arrived(mix_v.at[:, pl.ds(0, share), :], "mixx")
+            opposite_mix = mix_v.at[:, pl.ds(pl.multiple_of(across * share, 16), share), :]
+            send(opposite_mix, opposite_mix, "mixr", lat, twin)
         count_wait(meridian_v, lanes, sem(f"plane{k}.r"))
         meridian = meridian_v[:, :, lanes].reshape(side, width)
         coef_out[:, lanes] = jnp.dot(analysis_v[1 - core], meridian, preferred_element_type=f32)
@@ -415,9 +448,6 @@
             for r in range(2):
                 whole = gain_all[:, r].reshape(channels, half)
                 gain_v[r] = whole.T
-            arrived(mix_v.at[:, pl.ds(0, share), :], "mixx")
-            opposite_mix = mix_v.at[:, pl.ds(pl.multiple_of(across * share, 16), share), :]
-            send(opposite_mix, opposite_mix, "mixr", lat, twin)
         arrived(coef_in.at[:, lanes], f"coef{k}")
         own = coef_own[:, lanes]
         other = coef_in[:, lanes]
@@ -429,7 +459,7 @@
         gained_v[half : 2 * half, lanes] = (gain_real * imag + gain_imag * real).astype(bf16)
 
     def stage_mix(k):
-        base, width = spans[k]
+        base, width = spans_back[k]
         lanes = pl.ds(base, width)
         if k == 0:
             arrived(mix_v.at[:, pl.ds(0, share), :], "mixc")
@@ -445,7 +475,7 @@
         mixed_v[core, :, lanes] = jnp.where(core == 0, real, imag).astype(bf16)
 
     def stage_synthesis(k):
-        base, width = spans[k]
+        base, width = spans_back[k]
         lanes = pl.ds(base, width)
         arrived(mixed_v.at[1 - core, :, lanes], f"mixed{k}")
         mixed = mixed_v[:, :, lanes].reshape(2 * half, width)
@@ -472,7 +502,7 @@
             back_v[slot, :, lanes] = cycle_v[plane, :, lanes]
 
     def stage_turn_back(k):
-        base, width = spans[k]
+        base, width = spans_back[k]
         lanes = pl.ds(base, width)
         count_wait(back_v, lanes, sem(f"plback{k}.r"))
         back = back_v[:, :, lanes].reshape(side, width)
@@ -493,13 +523,13 @@
         modes_all[core, z, :, lanes] = column_back[z, :, lanes]
 
     def stage_share(k):
-        base, width = spans[k]
+        base, width = spans_back[k]
         lanes = pl.ds(base, width)
         arrived(modes_all.at[core, pl.ds(0, depth - 1), :, lanes], f"rgback{k}")
         send(modes_all.at[core, :, :, lanes], modes_all.at[core, :, :, lanes], f"modes{k}", lat, twin)
 
     def stage_inverse(k):
-        base, width = spans[k]
+        base, width = spans_back[k]
         lanes = pl.ds(base, width)
         if k == 0:
             loads["inverse0"].wait()
@@ -515,7 +545,7 @@
     def finish(which, spectral):
         second = (first_v[which].astype(f32) + spectral).astype(bf16).astype(f32)
         scale = lax.rsqrt(jnp.mean(second * second, axis=-1, keepdims=True) + norm_eps)
-        normed_v[...] = (second * norm_ref[...] * scale).astype(bf16)
+        normed_v[...] = (second * norm_ref[...].reshape(1, channels) * scale).astype(bf16)
         total_v[...] = second
         hidden_width = expand_v.shape[1]
         step = min(256, hidden_width)
@@ -526,25 +556,32 @@
             ).astype(bf16)
             total_v[...] += jnp.dot(hidden, reduce_v[columns, :], preferred_element_type=f32)
         out_ref[which] = total_v[0:sector, :].astype(bf16)
-
-    def pipeline(stages):
-        count = len(spans)
-        for beat in range(count + len(stages) - 1):
-            for depth_now, stage in enumerate(stages):
-                k = beat - depth_now
-                if 0 <= k < count:
-                    stage(k)
-
-    pipeline([stage_conv, stage_relay, stage_fourier, stage_turn, stage_analysis, stage_gain])
-    pipeline([stage_mix, stage_synthesis, stage_turn_back, stage_share, stage_inverse])
+        load(f"out{len(loads)}", out_ref.at[which], out_hbm.at[which])
+
+    def run(count, stages, lags):
+        for beat in range(count + max(lags)):
+            for stage, lag in reversed(list(zip(stages, lags))):
+                if 0 <= beat - lag < count:
+                    stage(beat - lag)
+
+    count = len(spans)
+    run(count, [stage_conv, stage_relay, stage_fourier], front_lags)
+    send_weights()
+    run(count, [stage_turn, stage_analysis, stage_gain], [0, count, 2 * count])
+    count = len(spans_back)
+    late = [stage_mix, stage_synthesis, stage_turn_back, stage_share, stage_inverse]
+    run(count, late, [0, count, 2 * count, 3 * count, 3 * count + 1])
 
     loads["expand"].wait()
     loads["reduce"].wait()
     finish(x_low, spectral_own[...])
-    for k, (base, width) in enumerate(spans):
+    for k, (base, width) in enumerate(spans_back):
         arrived(spectral_in.at[:, pl.ds(base, width)], f"spec{k}")
     finish(1 - x_low, spectral_in[...].astype(f32))
 
+    for name, copy in loads.items():
+        if name.startswith("out"):
+            copy.wait()
     left(edge_in, "edge")
     left(mix_v.at[:, pl.ds(0, share), :], "mixx")
     left(mix_v.at[:, pl.ds(0, share), :], "mixc")
@@ -558,6 +595,8 @@
         left(column_v.at[pl.ds(0, depth - 1), :, lanes], f"ring{k}")
         count_wait(meridian_v, lanes, sem(f"plane{k}.s"))
         left(coef_in.at[:, lanes], f"coef{k}")
+    for k, (base, width) in enumerate(spans_back):
+        lanes = pl.ds(base, width)
         left(mixed_out.at[:, lanes], f"mixed{k}")
         count_wait(back_v, lanes, sem(f"plback{k}.s"))
         left(column_v.at[pl.ds(0, depth - 1), :, lanes], f"rgback{k}")
@@ -565,13 +604,15 @@
         left(spectral_out.at[:, lanes], f"spec{k}")
 
 
-def spans_of(channels, pieces):
-    tiles = channels // 128
-    cuts = [tiles * i // pieces for i in range(pieces + 1)]
-    return [(128 * a, 128 * (b - a)) for a, b in zip(cuts, cuts[1:])]
-
-
-chunk_count = 1
+def spans_of(tiles):
+    edges = np.concatenate([[0], np.cumsum(tiles)]) * 128
+    return [(int(a), int(b - a)) for a, b in zip(edges, edges[1:])]
+
+
+front_tiles = (1, 2, 2)
+back_tiles = (2, 2, 1)
+halo_ahead = 2
+front_lags = (0, 1, 2)
 
 
 def shards(
@@ -594,16 +635,19 @@
     half = degrees // 2
     share = channels // 4
     hidden_width = expand_weight.shape[1]
-    spans = spans_of(channels, chunk_count)
+    spans, spans_back = spans_of(front_tiles), spans_of(back_tiles)
     forward, inverse = fourier_tables(sector, padded, degrees, rings, depth)
     rows = jnp.asarray(latitude_rows(lat_total, rings, depth))
     anywhere = pl.BlockSpec(memory_space=pl.ANY)
-    vmem = pl.BlockSpec(memory_space=pltpu.VMEM)
     scratch = [
+        (conv_weight.shape, f32),
+        (norm_gain.shape, f32),
+        (rows.shape, f32),
+        (grid_state.shape, bf16),
         ((2, sector, channels), bf16),
         ((2, sector, channels), bf16),
-        ((2, 2, edge_rows, channels), bf16),
-        ((2, 4, edge_rows, channels), bf16),
+        ((2, edge_rows, 128), bf16),
+        ((2, 3, edge_rows, 128), bf16),
         ((4, -(-(sector + 16) // 8) * 8, channels), f32),
         ((2, padded, channels), bf16),
         ((4, padded, channels), bf16),
@@ -642,14 +686,14 @@
         ((lat_total, degrees), bf16),
     ]
     return pl.pallas_call(
-        functools.partial(block_kernel, rings, depth, spans),
+        functools.partial(block_kernel, rings, depth, spans, spans_back),
         out_shape=jax.ShapeDtypeStruct(grid_state.shape, bf16),
-        in_specs=[anywhere, vmem, anywhere, anywhere, vmem] + [anywhere] * 4 + [vmem],
-        out_specs=vmem,
+        in_specs=[anywhere] * 10,
+        out_specs=anywhere,
         scratch_shapes=[pltpu.VMEM(*s) for s in scratch]
         + [
-            pltpu.SemaphoreType.DMA((10 + 24 * len(spans),)),
-            pltpu.SemaphoreType.DMA((9,)),
+            pltpu.SemaphoreType.DMA((10 + 14 * len(spans) + 10 * len(spans_back),)),
+            pltpu.SemaphoreType.DMA((14,)),
         ],
         compiler_params=pltpu.CompilerParams(
             collective_id=0, has_side_effects=True, vmem_limit_bytes=60 * 1024 * 1024
@@ -660,7 +704,7 @@
         conv_weight,
         jnp.swapaxes(spectral_gain, 1, 2),
         jnp.swapaxes(spectral_weight, 1, 2),
-        norm_gain.reshape(1, channels),
+        norm_gain,
         expand_weight,
         reduce_weight,
         forward,

time: 112 us -> 92.4 us (0.83)
  Pallas kernels: 106 us -> 88.2 us
  local copies, waits for them, and re-layouts: 5.25 us -> 3.99 us
    pallas_call x1, Pallas kernels: 106 us -> 88.2 us  [shards(): pl.pallas_call(functools.partial(block_kernel, rings, depth, spans, spans...]
    reshape x1 -> x0, local copies, waits for them, and re-layouts: 1.27 us -> none  [shards(): norm_gain.reshape(1, channels)]
where the time goes in v3:
time: 92.4 us; the launch traced here: 92.2 us
  Pallas kernels  88.2 us (95%)
  local copies, waits for them, and re-layouts  3.99 us (4%)
    pallas_call x1, Pallas kernels, shards(): pl.pallas_call(functools.partial(block_kernel, rings, depth, spans, spans...  88.2 us
    pallas_call x1, local copies, waits for them, and re-layouts, shards(): pl.pallas_call(functools.partial(block_kernel, rings, depth, spans, spans...  2.15 us

profile of v3, /device:TPU:1, one launch (start us, length us, event | category | flops | bytes accessed | tf_op | source)
XLA Modules:
  0.0 92.2 jit_solution(11439033327428647209)
XLA Ops:
  0.0 1.8 %copy.11.grid_hbm = bf16[2,180,640]{2,1,0:T(8,128)(2,1)} copy(bf16[2,180,640]{2,0,1:T(2,128)(2,1)} %param.10) | data formatting | bytes 921600 | tf_op args[0]
  1.8 88.2 %block_pair.1 = bf16[2,180,640]{2,1,0:T(8,128)(2,1)} custom-call(bf16[2,180,640]{2,1,0:T(8,128)(2,1)} %copy.11.grid_hbm, f32[3,3,640]{2,1,0:T(4,128)} %conv_hbm.1, f32[2,160,256]{2,1,0:T(8,128)} %bitcast.3, bf16[2,160,640]{2,1,0:T(8,128)(2,1)} %bitcast.2, f32[640]{0:T(1024)} %norm_hbm.1, bf16[640,1280]{1,0:T(8,128)(2,1)} %expand_hbm.1, ...), custom_call_target="tpu_custom_call" | custom-call | tf_op jit(solution)/shard_map/block_pair/pallas_call | solution.py:688
  90.1 2.1 %copy.12 = bf16[2,180,640]{2,0,1:T(2,128)(2,1)} copy(bf16[2,180,640]{2,1,0:T(8,128)(2,1)} %block_pair.1) | data formatting | bytes 921600 | tf_op jit(solution)/shard_map/block_pair/pallas_call | solution.py:688

commit v4 on v3

--- a/solution.py
+++ b/solution.py
@@ -16,6 +16,14 @@
 bf16 = jnp.bfloat16
 f32 = jnp.float32
 MESH = pl.DeviceIdType.MESH
+
+
+def div(a, b):
+    return lax.div(a, jnp.int32(b))
+
+
+def rem(a, b):
+    return lax.rem(a, jnp.int32(b))
 
 
 def cycle_of_row(rings, depth):
@@ -110,7 +118,9 @@
     conv_ref,
     norm_ref,
     rows_ref,
+    done_v,
     out_ref,
+    raw_v,
     grid_v,
     halo_v,
     edge_out,
@@ -153,6 +163,7 @@
     synthesis_v,
     sems,
     local_sems,
+    far_sems,
 ):
     sector, channels = grid_v.shape[1:]
     padded = first_v.shape[1]
@@ -162,22 +173,22 @@
     half = coef_own.shape[0]
     lat = lax.axis_index("lat")
     lon = lax.axis_index("lon")
-    x_high = lat % 2
-    z = (lat // 2) % depth
-    y = lat // (2 * depth)
-    x_low = lon // 2
-    core = lon % 2
+    x_high = rem(lat, 2)
+    z = rem(div(lat, 2), depth)
+    y = div(lat, 2 * depth)
+    x_low = div(lon, 2)
+    core = rem(lon, 2)
     plane = 4 * y + 2 * x_high + x_low
     slot = (2 * y + x_high) * 2 + core
     order = plane * depth + z
     twin = lon + 1 - 2 * core
-    across = (lon + 2) % 4
+    across = rem(lon + 2, 4)
     opposite = 3 - lon
-    lat_up = (lat + 1) % lat_count
-    lat_down = (lat + lat_count - 1) % lat_count
+    lat_up = rem(lat + 1, lat_count)
+    lat_down = rem(lat + lat_count - 1, lat_count)
     lat_pair = lat + 1 - 2 * x_high
-    lon_up = (lon + 1) % 4
-    lon_down = (lon + 3) % 4
+    lon_up = rem(lon + 1, 4)
+    lon_down = rem(lon + 3, 4)
     diagonal = core == x_low
 
     names = {}
@@ -208,48 +219,19 @@
         wait(ref, sem(name + ".s"))
 
     def z_offset(i):
-        return depth // 2 + (1 - 2 * (i % 2)) * ((i + 1) // 2)
+        return depth // 2 + (1 - 2 * rem(i, 2)) * div(i + 1, 2)
 
     def ring_peer(i):
-        return (z + z_offset(i)) % depth
+        return rem(z + z_offset(i), depth)
 
     def lat_of(y_to, z_to, high_to):
         return (y_to * depth + z_to) * 2 + high_to
 
     def order_peer(i):
-        return lat_of(i // 4, z, (i // 2) % 2), 2 * core + i % 2
+        return lat_of(div(i, 4), z, rem(div(i, 2), 2)), 2 * core + rem(i, 2)
 
     def cycle_peer(i):
-        return lat_of(i // 4, z, (i % 4) // 2), 2 * (i % 2) + x_low
-
-    barrier = pltpu.get_barrier_semaphore()
-
-    def greet(lat_to, lon_to):
-        pl.semaphore_signal(
-            barrier, inc=1, device_id={"lat": lat_to, "lon": lon_to}, device_id_type=MESH
-        )
-
-    for lat_to in (lat_up, lat_down):
-        for lon_to in (lon, lon_up, lon_down):
-            greet(lat_to, lon_to)
-    greet(lat, lon_up)
-    greet(lat, lon_down)
-    greet(lat, across)
-    greet(lat_pair, across)
-    greet(lat_pair, opposite)
-
-    @pl.loop(0, depth - 1)
-    def _(i):
-        greet(lat_of(y, ring_peer(i), x_high), lon)
-
-    @pl.loop(0, swap_rows)
-    def _(i):
-        for peer in (order_peer, cycle_peer):
-            lat_to, lon_to = peer(i)
-
-            @pl.when(jnp.logical_or(lat_to != lat, lon_to != lon))
-            def _():
-                greet(lat_to, lon_to)
+        return lat_of(div(i, 4), z, rem(div(i, 2), 2)), 2 * rem(i, 2) + x_low
 
     loads = {}
 
@@ -258,7 +240,7 @@
         copy.start()
         loads[name] = copy
 
-    load("grid", grid_hbm, grid_v)
+    load("grid", grid_hbm, raw_v)
     load("rows", rows_hbm, rows_ref)
     load("conv", conv_hbm, conv_ref)
     load("norm", norm_hbm, norm_ref)
@@ -272,7 +254,37 @@
     load("expand", expand_hbm, expand_v)
     load("reduce", reduce_hbm, reduce_v)
 
+    barrier = pltpu.get_barrier_semaphore()
+
+    def greet(lat_to, lon_to):
+        pl.semaphore_signal(
+            barrier, inc=1, device_id={"lat": lat_to, "lon": lon_to}, device_id_type=MESH
+        )
+
+    for lat_to in (lat_up, lat_down):
+        for lon_to in (lon, lon_up, lon_down):
+            greet(lat_to, lon_to)
+    greet(lat, lon_up)
+    greet(lat, lon_down)
+    greet(lat, across)
+    greet(lat_pair, across)
+    greet(lat_pair, opposite)
+
+    for step in (1, depth - 1):
+        greet(lat_of(y, rem(z + step, depth), x_high), lon)
+
+    @pl.loop(0, swap_rows)
+    def _(i):
+        for peer in (order_peer, cycle_peer):
+            lat_to, lon_to = peer(i)
+
+            @pl.when(jnp.logical_or(lat_to != lat, lon_to != lon))
+            def _():
+                greet(lat_to, lon_to)
+
     loads["grid"].wait()
+    for t in range(2):
+        grid_v[t] = raw_v[:, t, :]
     blank = jnp.zeros((8 - channels // 128, 128), f32)
     for side, at in ((0, 0), (1, sector - 8)):
         pieces = []
@@ -280,8 +292,24 @@
             line = grid_v[t, at : at + 8, :].astype(f32)[7 * side : 7 * side + 1]
             pieces += [line[:, base : base + 128] for base in range(0, channels, 128)] + [blank]
         edge_out[side] = jnp.concatenate(pieces, axis=0).astype(bf16)
-    pl.semaphore_wait(barrier, 11 + depth - 1 + 2 * swap_rows - 2 * diagonal.astype(jnp.int32))
-
+    pl.semaphore_wait(barrier, 13 + 2 * swap_rows - 2 * diagonal.astype(jnp.int32))
+
+    far_steps = [2**i for i in range(depth.bit_length()) if 2**i < depth // 2]
+
+    def tell(i):
+        for step in (far_steps[i], depth - far_steps[i]):
+            pl.semaphore_signal(
+                far_sems.at[i],
+                inc=1,
+                device_id={"lat": lat_of(y, rem(z + step, depth), x_high), "lon": lon},
+                device_id_type=MESH,
+            )
+
+    def hear(i):
+        pl.semaphore_wait(far_sems.at[i], 2)
+
+    if far_steps:
+        tell(0)
     for side, lon_to in ((0, lon_down), (1, lon_up)):
         for source, lat_to in ((0, lat_up), (1, lat), (2, lat_down)):
             send(edge_out.at[side], edge_in.at[side, source], "edge", lat_to, lon_to)
@@ -308,6 +336,10 @@
     table = table_v[...]
     analysis_v[...] = (table * rows_ref[2:3, :]).astype(bf16).reshape(analysis_v.shape)
     synthesis_v[...] = table.T.astype(bf16)
+
+    for i in range(1, len(far_steps)):
+        hear(i - 1)
+        tell(i)
 
     above = (lat > 0).astype(f32)
     below = (lat < lat_count - 1).astype(f32)
@@ -372,6 +404,8 @@
         lanes = pl.ds(base, width)
         if k == 0:
             loads["forward"].wait()
+            if far_steps:
+                hear(len(far_steps) - 1)
         arrived(circle_v.at[twin, :, lanes], f"lonc{k}")
         arrived(circle_v.at[opposite, :, lanes], f"lonr{k}")
         circle = circle_v[:, :, lanes].reshape(4 * padded, width)
@@ -401,7 +435,7 @@
 
         @pl.loop(0, swap_rows)
         def _(i):
-            to = (slot + i) % swap_rows
+            to = rem(slot + i, swap_rows)
             lat_to, lon_to = order_peer(to)
 
             @pl.when(jnp.logical_or(lat_to != lat, lon_to != lon))
@@ -484,7 +518,7 @@
 
         @pl.loop(0, swap_rows)
         def _(i):
-            to = (plane + i) % swap_rows
+            to = rem(plane + i, swap_rows)
             lat_to, lon_to = cycle_peer(to)
 
             @pl.when(jnp.logical_or(lat_to != lat, lon_to != lon))
@@ -555,8 +589,7 @@
                 jnp.dot(normed_v[...], expand_v[:, columns], preferred_element_type=f32)
             ).astype(bf16)
             total_v[...] += jnp.dot(hidden, reduce_v[columns, :], preferred_element_type=f32)
-        out_ref[which] = total_v[0:sector, :].astype(bf16)
-        load(f"out{len(loads)}", out_ref.at[which], out_hbm.at[which])
+        done_v[which] = total_v[...].astype(bf16)
 
     def run(count, stages, lags):
         for beat in range(count + max(lags)):
@@ -579,9 +612,10 @@
         arrived(spectral_in.at[:, pl.ds(base, width)], f"spec{k}")
     finish(1 - x_low, spectral_in[...].astype(f32))
 
-    for name, copy in loads.items():
-        if name.startswith("out"):
-            copy.wait()
+    for t in range(2):
+        out_ref[:, t, :] = done_v[t, 0:sector, :]
+    load("out", out_ref, out_hbm)
+    loads["out"].wait()
     left(edge_in, "edge")
     left(mix_v.at[:, pl.ds(0, share), :], "mixx")
     left(mix_v.at[:, pl.ds(0, share), :], "mixc")
@@ -643,7 +677,9 @@
         (conv_weight.shape, f32),
         (norm_gain.shape, f32),
         (rows.shape, f32),
-        (grid_state.shape, bf16),
+        ((2, padded, channels), bf16),
+        ((sector, 2, channels), bf16),
+        ((sector, 2, channels), bf16),
         ((2, sector, channels), bf16),
         ((2, sector, channels), bf16),
         ((2, edge_rows, 128), bf16),
@@ -685,22 +721,23 @@
         ((2, half, lat_total), bf16),
         ((lat_total, degrees), bf16),
     ]
-    return pl.pallas_call(
+    block_output = pl.pallas_call(
         functools.partial(block_kernel, rings, depth, spans, spans_back),
-        out_shape=jax.ShapeDtypeStruct(grid_state.shape, bf16),
+        out_shape=jax.ShapeDtypeStruct((sector, 2, channels), bf16),
         in_specs=[anywhere] * 10,
         out_specs=anywhere,
         scratch_shapes=[pltpu.VMEM(*s) for s in scratch]
         + [
             pltpu.SemaphoreType.DMA((10 + 14 * len(spans) + 10 * len(spans_back),)),
             pltpu.SemaphoreType.DMA((14,)),
+            pltpu.SemaphoreType.REGULAR((max(1, depth.bit_length()),)),
         ],
         compiler_params=pltpu.CompilerParams(
             collective_id=0, has_side_effects=True, vmem_limit_bytes=60 * 1024 * 1024
         ),
         name="block_pair",
     )(
-        grid_state,
+        jnp.swapaxes(grid_state, 0, 1),
         conv_weight,
         jnp.swapaxes(spectral_gain, 1, 2),
         jnp.swapaxes(spectral_weight, 1, 2),
@@ -711,6 +748,7 @@
         inverse,
         rows,
     )
+    return jnp.swapaxes(block_output, 0, 1)
 
 
 def solution(mesh):

time: 92.4 us -> 89.2 us (0.965)
  local copies, waits for them, and re-layouts: 3.99 us -> 2.11 us
  Pallas kernels: 88.2 us -> 87 us
    pallas_call x1 -> x0, local copies, waits for them, and re-layouts: 2.15 us -> none  [shards(): pl.pallas_call(functools.partial(block_kernel, rings, depth, spans, spans...]
    pallas_call x1, Pallas kernels: 88.2 us -> 87 us  [shards(): pl.pallas_call(functools.partial(block_kernel, rings, depth, spans, spans...]
where the time goes in v4:
time: 89.2 us; the launch traced here: 89.1 us
  Pallas kernels  87 us (98%)
  local copies, waits for them, and re-layouts  2.11 us (2%)
    pallas_call x1, Pallas kernels, shards(): pl.pallas_call(functools.partial(block_kernel, rings, depth, spans, spans...  87 us
    unnamed x1, local copies, waits for them, and re-layouts  2.11 us

profile of v4, /device:TPU:1, one launch (start us, length us, event | category | flops | bytes accessed | tf_op | source)
XLA Modules:
  0.0 89.1 jit_solution(17374311169550945616)
XLA Ops:
  0.0 87.0 %block_pair.1 = bf16[180,2,640]{2,1,0:T(2,128)(2,1)} custom-call(bf16[180,2,640]{2,1,0:T(2,128)(2,1)} %bitcast.5, f32[3,3,640]{2,1,0:T(4,128)} %conv_hbm.1, f32[2,160,256]{2,1,0:T(8,128)} %bitcast.7, bf16[2,160,640]{2,1,0:T(8,128)(2,1)} %bitcast.6, f32[640]{0:T(1024)} %norm_hbm.1, bf16[640,1280]{1,0:T(8,128)(2,1)} %expand_hbm.1, ...), custom_call_target="tpu_custom_call" | custom-call | tf_op jit(solution)/shard_map/block_pair/pallas_call | solution.py:724
  87.0 2.1 %copy.12 = bf16[2,180,640]{2,0,1:T(2,128)(2,1)} copy(bf16[2,180,640]{2,0,1:T(2,128)(2,1)} %bitcast.4) | data formatting | bytes 921600

commit v5 on v4

--- a/solution.py
+++ b/solution.py
@@ -378,16 +378,21 @@
         circle_v[lon, :, lanes] = first_v[x_low, :, lanes]
         if k + ahead < len(spans):
             stage_halo(k + ahead)
-
-    def send_weights():
+        if k == len(spans) - 1:
+            send_mix()
+
+    def send_mix():
         loads["mix"].wait()
-        loads["gain0"].wait()
-        loads["gain1"].wait()
-        gain_all[lon] = gain_part[core]
         rows = pl.ds(pl.multiple_of(lon * share, 16), share)
         for i, lat_to in ((0, lat_pair), (1, lat)):
             part = mix_v.at[i, rows, :]
             send(part, part, "mixx", lat_to, across)
+
+    def send_gain():
+        loads["gain0"].wait()
+        loads["gain1"].wait()
+        gain_all[lon] = gain_part[core]
+        for i, lat_to in ((0, lat_pair), (1, lat)):
             send(gain_part.at[core, i], gain_all.at[lon, i], "gain", lat_to, across)
             send(gain_part.at[1 - core, i], gain_all.at[lon, i], "gain", lat_to, opposite)
         send(mix_own, mix_own, "mixc", lat, twin)
@@ -451,6 +456,9 @@
         @pl.when(diagonal)
         def _():
             meridian_v[plane, :, lanes] = turned_v[slot, :, lanes]
+
+        if k == 0:
+            send_gain()
 
     def count_wait(ref, lanes, semaphore):
         @pl.when(diagonal)
@@ -599,8 +607,7 @@
 
     count = len(spans)
     run(count, [stage_conv, stage_relay, stage_fourier], front_lags)
-    send_weights()
-    run(count, [stage_turn, stage_analysis, stage_gain], [0, count, 2 * count])
+    run(count, [stage_turn, stage_analysis, stage_gain], middle_lags)
     count = len(spans_back)
     late = [stage_mix, stage_synthesis, stage_turn_back, stage_share, stage_inverse]
     run(count, late, [0, count, 2 * count, 3 * count, 3 * count + 1])
@@ -647,6 +654,7 @@
 back_tiles = (2, 2, 1)
 halo_ahead = 2
 front_lags = (0, 1, 2)
+middle_lags = (0, 3, 6)
 
 
 def shards(

time: 89.2 us -> 88.5 us (level)
  no operation moved by 1% of the time
where the time goes in v5:
time: 88.5 us; the launch traced here: 88.3 us
  Pallas kernels  86.2 us (97%)
  local copies, waits for them, and re-layouts  2.11 us (2%)
    pallas_call x1, Pallas kernels, shards(): pl.pallas_call(functools.partial(block_kernel, rings, depth, spans, spans...  86.2 us
    unnamed x1, local copies, waits for them, and re-layouts  2.11 us

profile of v5, /device:TPU:1, one launch (start us, length us, event | category | flops | bytes accessed | tf_op | source)
XLA Modules:
  0.0 88.3 jit_solution(11049385412497147054)
XLA Ops:
  0.0 86.2 %block_pair.1 = bf16[180,2,640]{2,1,0:T(2,128)(2,1)} custom-call(bf16[180,2,640]{2,1,0:T(2,128)(2,1)} %bitcast.5, f32[3,3,640]{2,1,0:T(4,128)} %conv_hbm.1, f32[2,160,256]{2,1,0:T(8,128)} %bitcast.7, bf16[2,160,640]{2,1,0:T(8,128)(2,1)} %bitcast.6, f32[640]{0:T(1024)} %norm_hbm.1, bf16[640,1280]{1,0:T(8,128)(2,1)} %expand_hbm.1, ...), custom_call_target="tpu_custom_call" | custom-call | tf_op jit(solution)/shard_map/block_pair/pallas_call | solution.py:732
  86.2 2.1 %copy.12 = bf16[2,180,640]{2,0,1:T(2,128)(2,1)} copy(bf16[2,180,640]{2,0,1:T(2,128)(2,1)} %bitcast.4) | data formatting | bytes 921600
